TPU v7x, 32 devices: a whole 2x2x4 slice. The times are simulated.
32 devices in a mesh: img: 4 (over y, core), txt: 8 (over z, x).
Axes of the slice: x: 2, y: 2, z: 4, core: 2. Of those that a mesh axis runs over, the one named last changes fastest.
Arguments:
- queries: bfloat16 [1, 5120, 8192], P(None, 'txt', 'img'), may hold values from -128 to 128
- visual_keys: bfloat16 [1, 512, 8192], P(None, 'img'), may hold values from -5 to 5
- visual_values: bfloat16 [1, 512, 8192], P(None, 'img'), may hold values from -6 to 6
- out_grad: bfloat16 [1, 5120, 8192], P(None, 'txt', 'img'), may hold values from -6 to 6
- gate_value: float32 [1, 64], P(None, 'img'), may hold values from -1.5 to 1.5
- image_order: int32 [1, 8], replicated, may hold values from 0 to 7, as said below
- image_seen: int32 [5120], P('txt'), may hold values from 1 to 8
Outputs:
- query_grad: bfloat16 [1, 5120, 8192], P(None, 'txt', 'img')
- key_grad: float32 [1, 512, 8192], P(None, 'txt', 'img')
- value_grad: float32 [1, 512, 8192], P(None, 'txt', 'img')
Inputs may be any that keep to these rules, and one draw needn't show every extreme that they name: `image_order`: each row names every image of 0 to 7 once.
All inputs are finite; a program needn't handle non-finite values.
Results may differ from a plain program's by a relative error of at most 0.0058.
Values may be sent and summed in bfloat16 or wider, within the bound.
A program may use at most 128 MiB of HBM per device.

v0:
```python
import functools
import math

import jax
import jax.numpy as jnp
from jax import lax
from jax.experimental import pallas as pl
from jax.experimental.pallas import tpu as pltpu
from jax.sharding import PartitionSpec as P

NT = (((1,), (1,)), ((), ()))
TN = (((0,), (0,)), ((), ()))
NN = (((1,), (0,)), ((), ()))


def matmul(left, right, dims):
    return lax.dot_general(left, right, dims, preferred_element_type=jnp.float32)


def head_grads(query, gated, key, value, bias):
    rows, tokens = key.shape[0], query.shape[0]
    images = bias.shape[0]
    scale = 1.0 / math.sqrt(query.shape[1])
    scores = matmul(key, query, NT) * (scale * math.log2(math.e))
    masked = (scores.reshape(images, rows // images, tokens) + bias[:, None, :]).reshape(rows, tokens)
    exponent = jnp.exp2(masked - jnp.max(masked, axis=0, keepdims=True))
    weights = exponent * (1.0 / jnp.sum(exponent, axis=0, keepdims=True))
    weight_half = weights.astype(jnp.bfloat16)
    weight_grad = matmul(value, gated, NT)
    delta = jnp.sum(weight_half.astype(jnp.float32) * weight_grad, axis=0, keepdims=True)
    score_half = (weights * (weight_grad - delta)).astype(jnp.bfloat16)
    query_grad = (matmul(key, score_half, TN) * scale).T
    key_grad = matmul(score_half, query, NN) * scale
    value_grad = matmul(weight_half, gated, NN)
    return query_grad, key_grad, value_grad


def kernel(images_n, sides, order_ref, gate_ref, seen_ref, query_ref, grad_ref, key_ref, value_ref,
           out_ref, key_out, value_out,
           bias, latents, part, pair_out, pair_in, far_out, far_in,
           latent_send, latent_recv, pair_send, pair_recv, far_send, far_recv):
    head = pl.program_id(0)
    heads = pl.num_programs(0)
    width = query_ref.shape[1]
    owned = key_ref.shape[0]
    me = lax.axis_index("img")
    place = lax.axis_index("txt")
    mine = place // 2
    side = place % 2
    other = 1 - side
    partner = {"txt": mine * 2 + other}

    def latent_copy(source, index, slot, off):
        owner = (me + off) % images_n
        column = pl.multiple_of((owner * heads + index) * width, width)
        view = source.at[:, pl.ds(column, width)]
        target = latents.at[index, slot, pl.ds(pl.multiple_of(me * owned, owned), owned), :]
        if off == 0:
            return pltpu.make_async_copy(view, target, latent_recv.at[index])
        return pltpu.make_async_remote_copy(
            src_ref=view, dst_ref=target, send_sem=latent_send.at[index],
            recv_sem=latent_recv.at[index], device_id={"img": owner},
            device_id_type=pl.DeviceIdType.MESH)

    def pair_copy(index):
        return pltpu.make_async_remote_copy(
            src_ref=pair_out.at[index], dst_ref=pair_in.at[index],
            send_sem=pair_send.at[index], recv_sem=pair_recv.at[index],
            device_id=partner, device_id_type=pl.DeviceIdType.MESH)

    def far_copy(index, off):
        there = (mine + off) % sides
        return pltpu.make_async_remote_copy(
            src_ref=far_out.at[index, off - 1], dst_ref=far_in.at[index, off - 1],
            send_sem=far_send.at[index], recv_sem=far_recv.at[index],
            device_id={"txt": there * 2 + side}, device_id_type=pl.DeviceIdType.MESH)

    def drain(ref, sem):
        pltpu.make_async_copy(ref, ref, sem).wait()

    def columns(index):
        return pl.ds(pl.multiple_of(index * width, width), width)

    @pl.when(head == 0)
    def _():
        barrier = pltpu.get_barrier_semaphore()
        peers = [{"img": (me + off) % images_n} for off in range(1, images_n)] + [partner]
        peers += [{"txt": ((mine + off) % sides) * 2 + side} for off in range(1, sides)]
        for peer in peers:
            pl.semaphore_signal(barrier, inc=1, device_id=peer, device_id_type=pl.DeviceIdType.MESH)
        pl.semaphore_wait(barrier, len(peers))

        def send(index, carry):
            for off in list(range(1, images_n)) + [0]:
                latent_copy(key_ref, index, 0, off).start()
                latent_copy(value_ref, index, 1, off).start()
            return carry

        lax.fori_loop(0, heads, send, 0)
        seen = seen_ref[...].reshape(1, bias.shape[1])
        for i in range(order_ref.shape[1]):
            bias[pl.ds(i, 1), :] = jnp.where(seen > order_ref[0, i], 0.0, -1e30)

    def relay(index):
        pair_copy(index).wait_recv()
        slot = index % 2
        for off in range(1, sides):
            there = (mine + off) % sides
            for kind in range(2):
                far_out[index, off - 1, kind] = (
                    part[slot, kind, there * 2 + side]
                    + pair_in[index, kind, there].astype(jnp.float32)
                ).astype(jnp.bfloat16)
        for off in range(1, sides):
            far_copy(index, off).start()
        for kind, out in enumerate((key_out, value_out)):
            out[:, columns(index)] = (
                part[slot, kind, mine * 2 + side] + pair_in[index, kind, mine].astype(jnp.float32)
            )

    def finish(index):
        drain(far_in.at[index], far_recv.at[index])
        for kind, out in enumerate((key_out, value_out)):
            total = out[:, columns(index)]
            for off in range(1, sides):
                total = total + far_in[index, off - 1, kind].astype(jnp.float32)
            out[:, columns(index)] = total

    drain(latents.at[head], latent_recv.at[head])
    lane = lax.broadcasted_iota(jnp.int32, gate_ref.shape, 1)
    gate = jnp.sum(jnp.where(lane == head, gate_ref[...], 0.0), axis=1, keepdims=True)
    gated = (grad_ref[...].astype(jnp.float32) * jnp.tanh(gate)).astype(jnp.bfloat16)
    query_grad, key_grad, value_grad = head_grads(
        query_ref[...], gated, latents[head, 0], latents[head, 1], bias[...]
    )
    out_ref[...] = query_grad.astype(out_ref.dtype)
    now = head % 2
    shape = part.shape[2:]
    part[now, 0] = key_grad.reshape(shape)
    part[now, 1] = value_grad.reshape(shape)
    for kind in range(2):
        for there in range(sides):
            pair_out[head, kind, there] = part[now, kind, there * 2 + other].astype(jnp.bfloat16)
    pair_copy(head).start()

    @pl.when(head >= 1)
    def _():
        relay(head - 1)

    @pl.when(head >= 2)
    def _():
        finish(head - 2)

    @pl.when(head == heads - 1)
    def _():
        relay(heads - 1)
        finish(heads - 2)
        finish(heads - 1)

        def settle(index, carry):
            drain(latents.at[index, :, pl.ds(0, owned * (images_n - 1)), :], latent_send.at[index])
            pair_copy(index).wait_send()
            drain(far_out.at[index], far_send.at[index])
            return carry

        lax.fori_loop(0, heads, settle, 0)


def attention(images_n, texts_n, order, gate, seen, query, grad, key, value):
    tokens, width = query.shape
    heads = gate.shape[1]
    head_width = width // heads
    owned = key.shape[0]
    rows = owned * images_n
    sides = texts_n // 2
    share = rows // texts_n
    smem = pl.BlockSpec(memory_space=pltpu.SMEM)
    hbm = pl.BlockSpec(memory_space=pl.ANY)
    column = pl.BlockSpec((tokens, head_width), lambda h: (0, h))
    fixed = pl.BlockSpec((share, width), lambda h: (0, 0))
    half = jnp.bfloat16
    dma = pltpu.SemaphoreType.DMA((heads,))
    return pl.pallas_call(
        functools.partial(kernel, images_n, sides),
        grid=(heads,),
        in_specs=[smem, pl.BlockSpec((1, heads), lambda h: (0, 0)),
                  pl.BlockSpec((tokens,), lambda h: (0,)), column, column, hbm, hbm],
        out_specs=[column, fixed, fixed],
        out_shape=[jax.ShapeDtypeStruct((tokens, width), half)]
        + [jax.ShapeDtypeStruct((share, width), jnp.float32)] * 2,
        scratch_shapes=[
            pltpu.VMEM((order.shape[1], tokens), jnp.float32),
            pltpu.VMEM((heads, 2, rows, head_width), half),
            pltpu.VMEM((2, 2, texts_n, share, head_width), jnp.float32),
            pltpu.VMEM((heads, 2, sides, share, head_width), half),
            pltpu.VMEM((heads, 2, sides, share, head_width), half),
            pltpu.VMEM((heads, sides - 1, 2, share, head_width), half),
            pltpu.VMEM((heads, sides - 1, 2, share, head_width), half),
            dma, dma, dma, dma, dma, dma,
        ],
        compiler_params=pltpu.CompilerParams(
            vmem_limit_bytes=56 * 1024 * 1024, collective_id=0, has_side_effects=True
        ),
    )(order, gate, seen, query, grad, key, value)


def shards(images_n, texts_n, queries, visual_keys, visual_values, out_grad, gate_value, image_order, image_seen):
    query_grad, key_share, value_share = attention(
        images_n, texts_n, image_order, gate_value, image_seen,
        queries[0], out_grad[0], visual_keys[0], visual_values[0]
    )
    return (query_grad[None], key_share[None], value_share[None])


def solution(mesh):
    placed = (
        P(None, "txt", "img"),
        P(None, "img", None),
        P(None, "img", None),
        P(None, "txt", "img"),
        P(None, "img"),
        P(),
        P("txt"),
    )
    return jax.shard_map(
        functools.partial(shards, mesh.shape["img"], mesh.shape["txt"]),
        mesh=mesh,
        in_specs=placed,
        out_specs=(P(None, "txt", "img"), P(None, "txt", "img"), P(None, "txt", "img")),
        check_vma=False,
    )
```

profile of v0, /device:TPU:0, one launch (start us, length us, event | category | flops | bytes accessed | tf_op | source)
XLA Modules:
  0.0 84.8 jit_solution(762893362487167824)
XLA Ops:
  0.6 78.9 %shard_map.94 = (bf16[640,2048]{1,0:T(8,128)(2,1)}, f32[64,2048]{1,0:T(8,128)}, f32[64,2048]{1,0:T(8,128)}) custom-call(s32[1,8]{1,0:T(1,128)} %order_ref.1, f32[1,16]{1,0:T(1,128)} %gate_ref.1, s32[640]{0:T(1024)} %seen_ref.1, bf16[640,2048]{1,0:T(8,128)(2,1)} %bitcast.8, bf16[640,2048]{1,0:T(8,128)(2,1)} %bitcast.9, bf16[128,8192]{1,0:T(8,128)(2,1)} %bitcast.10, ...), custom_call_target="tpu_custom_call" | custom-call | tf_op jit(solution)/shard_map/pallas_call | solution.py:183
  79.5 0.0 copy-start.1
  79.5 0.0 copy-start
  79.6 3.6 %copy.13 = bf16[1,640,2048]{2,1,0:T(8,128)(2,1)} copy(bf16[1,640,2048]{2,1,0:T(8,128)(2,1)} %bitcast.7) | data formatting | bytes 5242880
  83.2 0.0 copy-done.1
  83.2 0.8 copy.14
  84.0 0.0 copy-done
  84.0 0.8 copy.15
Async XLA Ops:
  79.5 3.7 %copy-start.1 = (f32[64,2048]{1,0:T(8,128)S(1)}, f32[64,2048]{1,0:T(8,128)}, u32[]{:S(2)}) copy-start(f32[64,2048]{1,0:T(8,128)} %get-tuple-element.7) | copy-start | bytes 1572868
  79.5 4.5 %copy-start = (f32[64,2048]{1,0:T(8,128)S(1)}, f32[64,2048]{1,0:T(8,128)}, u32[]{:S(2)}) copy-start(f32[64,2048]{1,0:T(8,128)} %get-tuple-element.8) | copy-start | bytes 1572868
where the time goes:
time: 84.9 us; the launch traced here: 84.8 us
  Pallas kernels  78.9 us (93%)
  local copies, waits for them, and re-layouts  5.24 us (6%)
    pallas_call x1, Pallas kernels, attention(): pl.pallas_call(functools.partial(kernel, images_n, sides), grid=(heads,),...  78.9 us
    unnamed x7, local copies, waits for them, and re-layouts  5.24 us

commit v1 on v0

v1 whole, which is shorter than its diff:
```python
import functools
import math

import jax
import jax.numpy as jnp
from jax import lax
from jax.experimental import pallas as pl
from jax.experimental.pallas import tpu as pltpu
from jax.sharding import PartitionSpec as P

NT = (((1,), (1,)), ((), ()))
TN = (((0,), (0,)), ((), ()))
NN = (((1,), (0,)), ((), ()))
MESH = pl.DeviceIdType.MESH
LAGS = (2, 4, 6)


def matmul(left, right, dims):
    return lax.dot_general(left, right, dims, preferred_element_type=jnp.float32)


def head_grads(query, gated, key, value, bias):
    rows, tokens = key.shape[0], query.shape[0]
    images = bias.shape[0]
    scale = 1.0 / math.sqrt(query.shape[1])
    scores = matmul(key, query, NT) * (scale * math.log2(math.e))
    masked = (scores.reshape(images, rows // images, tokens) + bias[:, None, :]).reshape(rows, tokens)
    exponent = jnp.exp2(masked - jnp.max(masked, axis=0, keepdims=True))
    weights = exponent * (1.0 / jnp.sum(exponent, axis=0, keepdims=True))
    weight_half = weights.astype(jnp.bfloat16)
    weight_grad = matmul(value, gated, NT)
    delta = jnp.sum(weight_half.astype(jnp.float32) * weight_grad, axis=0, keepdims=True)
    score_half = (weights * (weight_grad - delta)).astype(jnp.bfloat16)
    query_grad = (matmul(key, score_half, TN) * scale).T
    key_grad = matmul(score_half, query, NN) * scale
    value_grad = matmul(weight_half, gated, NN)
    return query_grad, key_grad, value_grad


def kernel(images_n, sides, relief, order_ref, gate_ref, seen_ref, query_ref, grad_ref, key_ref, value_ref,
           out_ref, key_out, value_out,
           bias, queries, grads, latents, full, pair_out, pair_in, edge_out, edge_in, near_out, near_in,
           far_out, far_in,
           load_sem, near_sem, far_sem, latent_send, pair_send, pair_recv, line_send, edge_recv, near_recv,
           far_recv):
    heads = gate_ref.shape[1]
    width = queries.shape[2]
    owned = key_ref.shape[0]
    half = jnp.bfloat16
    pairs = sides // 2
    chips = images_n // 2
    me = lax.axis_index("img")
    place = lax.axis_index("txt")
    mine = place // 2
    side = place % 2
    other = 1 - side
    group = mine // 2
    parity = group % 2
    centre = jnp.where(group < pairs // 2, 1, 0) if pairs > 1 else 1
    inner = mine % 2 == centre
    outer = jnp.logical_not(inner)
    hub = group * 2 + centre
    rim = group * 2 + 1 - centre
    chip = me // 2
    sibling = chip * 2 + 1 - me % 2

    def at(z):
        return {"txt": z * 2 + side}

    def hub_of(g):
        return g * 2 + (jnp.where(g < pairs // 2, 1, 0) if pairs > 1 else 1)

    def columns(index):
        return pl.ds(pl.multiple_of(index * width, width), width)

    def remote(src, dst, send, recv, device):
        return pltpu.make_async_remote_copy(src_ref=src, dst_ref=dst, send_sem=send, recv_sem=recv,
                                            device_id=device, device_id_type=MESH)

    def drain(ref, sem):
        pltpu.make_async_copy(ref, ref, sem).wait()

    def rows_of(owner, count):
        return pl.ds(pl.multiple_of(owner * owned, owned), count * owned)

    takes = jnp.where(inner, parity, 1 - parity)

    def relieved(index):
        return jnp.logical_and(index >= 1, index <= 2 * relief)

    def fetched(index):
        return jnp.logical_or(jnp.logical_not(relieved(index)), (index + 1) % 2 == takes)

    def forwarder(index):
        return jnp.logical_and(inner, jnp.logical_and(relieved(index), fetched(index)))

    def foreign(index, off):
        return latents.at[index, :, rows_of(((chip + off) % chips) * 2, 2), :]

    def forward_copies(index):
        copies = []
        for device in (at(hub_of(group ^ 1)), at(rim)):
            for off in range(1, chips):
                view = foreign(index, off)
                copies.append(remote(view, view, latent_send.at[index], far_sem.at[index], device))
        return copies

    def drain_foreign(index):
        drain(latents.at[index, :, pl.ds(0, (images_n - 2) * owned), :], far_sem.at[index])

    def forward(m):
        index = 1 + 2 * m + parity

        @pl.when(jnp.logical_and(inner, m < relief))
        def _():
            drain_foreign(index)
            for copy in forward_copies(index):
                copy.start()

    def pair_copy(index):
        return remote(pair_out.at[index], pair_in.at[index], pair_send.at[index], pair_recv.at[index],
                      {"txt": mine * 2 + other})

    def edge_copy(index):
        return remote(edge_out.at[index], edge_in.at[index], line_send.at[index], edge_recv.at[index], at(hub))

    def near_copy(index):
        return remote(near_out.at[index], near_in.at[index], line_send.at[index], near_recv.at[index], at(rim))

    def far_copy(index, off, member):
        there = ((group + off) % pairs) * 2 + member
        return remote(far_out.at[index, off - 1, member], far_in.at[index, off - 1],
                      line_send.at[index], far_recv.at[index], at(there))

    barrier = pltpu.get_barrier_semaphore()

    def greet(device):
        pl.semaphore_signal(barrier, inc=1, device_id=device, device_id_type=MESH)

    for off in range(1, images_n):
        greet({"img": (me + off) % images_n})
    greet({"txt": mine * 2 + other})
    greet(at(mine ^ 1))
    for off in range(1, pairs):
        there = (group + off) % pairs
        greet(at(hub_of(there)))

        @pl.when(inner)
        def _():
            greet(at(there * 2 + 1 - (hub_of(there) - there * 2)))

    def load(index):
        return [pltpu.make_async_copy(ref.at[:, columns(index)], buf.at[index], load_sem.at[index])
                for ref, buf in ((query_ref, queries), (grad_ref, grads))]

    for copy in load(0):
        copy.start()
    pl.semaphore_wait(barrier, images_n - 1 + 2 + (pairs - 1) * jnp.where(inner, 2, 1))

    def send(index, carry):
        for slot, ref in enumerate((key_ref, value_ref)):
            target = latents.at[index, slot, rows_of(me, 1), :]
            remote(ref.at[:, columns(sibling * heads + index)], target,
                   latent_send.at[index], near_sem.at[index], {"img": sibling}).start()
            pltpu.make_async_copy(ref.at[:, columns(me * heads + index)], target, near_sem.at[index]).start()

        @pl.when(fetched(index))
        def _():
            for off in range(1, chips):
                for core in range(2):
                    owner = ((chip + off) % chips) * 2 + core
                    for slot, ref in enumerate((key_ref, value_ref)):
                        remote(ref.at[:, columns(owner * heads + index)],
                               latents.at[index, slot, rows_of(me, 1), :],
                               latent_send.at[index], far_sem.at[index], {"img": owner}).start()

        @pl.when(index > 0)
        def _():
            for copy in load(index):
                copy.start()

        return carry

    lax.fori_loop(0, heads, send, 0)
    seen = seen_ref[...].reshape(1, bias.shape[1])
    for i in range(order_ref.shape[1]):
        bias[pl.ds(i, 1), :] = jnp.where(seen > order_ref[0, i], 0.0, -1e30)

    outs = (key_out, value_out)

    def compute(index):
        drain(latents.at[index, :, pl.ds(0, 2 * owned), :], near_sem.at[index])

        @pl.when(index == 1)
        def _():
            forward(0)

        @pl.when(jnp.logical_not(forwarder(index)))
        def _():
            drain_foreign(index)

        @pl.when(jnp.logical_and(index >= 2, index % 2 == 0))
        def _():
            forward(index // 2)

        for copy in load(index):
            copy.wait()
        lane = lax.broadcasted_iota(jnp.int32, gate_ref.shape, 1)
        gate = jnp.sum(jnp.where(lane == index, gate_ref[...], 0.0), axis=1, keepdims=True)
        gated = (grads[index].astype(jnp.float32) * jnp.tanh(gate)).astype(half)
        query_grad, key_grad, value_grad = head_grads(
            queries[index], gated, latents[index, 0], latents[index, 1], bias[...]
        )
        out_ref[:, columns(index)] = query_grad.astype(out_ref.dtype)
        shape = full.shape[2:]
        full[index, 0] = key_grad.reshape(shape)
        full[index, 1] = value_grad.reshape(shape)
        for kind in range(2):
            for z in range(sides):
                pair_out[index, kind, z] = full[index, kind, z * 2 + other].astype(half)
        pair_copy(index).start()

    def line(index, kind, z):
        return full[index, kind, z * 2 + side] + pair_in[index, kind, z].astype(jnp.float32)

    def relay(index):
        pair_copy(index).wait_recv()

        @pl.when(outer)
        def _():
            for j in range(sides - 1):
                for kind in range(2):
                    edge_out[index, j, kind] = line(index, kind, (rim + 1 + j) % sides).astype(half)
            edge_copy(index).start()

        @pl.when(inner)
        def _():
            for kind in range(2):
                near_out[index, kind] = line(index, kind, rim).astype(half)
            near_copy(index).start()

        for kind, out in enumerate(outs):
            out[:, columns(index)] = line(index, kind, mine)

    def merge(index):
        @pl.when(inner)
        def _():
            edge_copy(index).wait_recv()
            for off in range(1, pairs):
                for member in range(2):
                    z = ((group + off) % pairs) * 2 + member
                    for kind in range(2):
                        far_out[index, off - 1, member, kind] = (
                            line(index, kind, z)
                            + edge_in[index, (z - rim - 1 + sides) % sides, kind].astype(jnp.float32)
                        ).astype(half)
                    far_copy(index, off, member).start()
            for kind, out in enumerate(outs):
                out[:, columns(index)] += edge_in[index, (hub - rim - 1 + sides) % sides, kind].astype(jnp.float32)

        @pl.when(outer)
        def _():
            near_copy(index).wait_recv()
            for kind, out in enumerate(outs):
                out[:, columns(index)] += near_in[index, kind].astype(jnp.float32)

    def finish(index):
        drain(far_in.at[index], far_recv.at[index])
        for kind, out in enumerate(outs):
            total = out[:, columns(index)]
            for off in range(1, pairs):
                total = total + far_in[index, off - 1, kind].astype(jnp.float32)
            out[:, columns(index)] = total

    def step(i, carry):
        @pl.when(i < heads)
        def _():
            compute(i)

        stages = [relay, merge] + ([finish] if pairs > 1 else [])
        for lag, stage in zip(LAGS, stages):
            @pl.when(jnp.logical_and(i >= lag, i < heads + lag))
            def _(lag=lag, stage=stage):
                stage(i - lag)

        return carry

    lax.fori_loop(0, heads + LAGS[-1], step, 0)

    def settle(index, carry):
        drain(latents.at[index, :, pl.ds(0, owned), :], latent_send.at[index])

        @pl.when(fetched(index))
        def _():
            drain(latents.at[index, :, pl.ds(0, (images_n - 2) * owned), :], latent_send.at[index])

        @pl.when(forwarder(index))
        def _():
            for copy in forward_copies(index):
                copy.wait_send()

        pair_copy(index).wait_send()

        @pl.when(outer)
        def _():
            edge_copy(index).wait_send()

        @pl.when(inner)
        def _():
            near_copy(index).wait_send()
            for off in range(1, pairs):
                for member in range(2):
                    far_copy(index, off, member).wait_send()

        return carry

    lax.fori_loop(0, heads, settle, 0)


def attention(images_n, texts_n, order, gate, seen, query, grad, key, value):
    tokens, width = query.shape
    heads = gate.shape[1]
    head_width = width // heads
    rows = key.shape[0] * images_n
    sides = texts_n // 2
    pairs = sides // 2
    share = rows // texts_n
    relief = heads // 4 if pairs % 2 == 0 and images_n > 2 else 0
    smem = pl.BlockSpec(memory_space=pltpu.SMEM)
    vmem = pl.BlockSpec(memory_space=pltpu.VMEM)
    hbm = pl.BlockSpec(memory_space=pl.ANY)
    half = jnp.bfloat16
    dma = pltpu.SemaphoreType.DMA((heads,))
    return pl.pallas_call(
        functools.partial(kernel, images_n, sides, relief),
        in_specs=[smem, vmem, vmem, hbm, hbm, hbm, hbm],
        out_specs=[vmem, vmem, vmem],
        out_shape=[pltpu.VMEM((tokens, width), half)] + [pltpu.VMEM((share, width), jnp.float32)] * 2,
        scratch_shapes=[
            pltpu.VMEM((order.shape[1], tokens), jnp.float32),
            pltpu.VMEM((heads, tokens, head_width), half),
            pltpu.VMEM((heads, tokens, head_width), half),
            pltpu.VMEM((heads, 2, rows, head_width), half),
            pltpu.VMEM((heads, 2, texts_n, share, head_width), jnp.float32),
            pltpu.VMEM((heads, 2, sides, share, head_width), half),
            pltpu.VMEM((heads, 2, sides, share, head_width), half),
            pltpu.VMEM((heads, sides - 1, 2, share, head_width), half),
            pltpu.VMEM((heads, sides - 1, 2, share, head_width), half),
            pltpu.VMEM((heads, 2, share, head_width), half),
            pltpu.VMEM((heads, 2, share, head_width), half),
            pltpu.VMEM((heads, max(pairs - 1, 1), 2, 2, share, head_width), half),
            pltpu.VMEM((heads, max(pairs - 1, 1), 2, share, head_width), half),
        ] + [dma] * 10,
        compiler_params=pltpu.CompilerParams(
            vmem_limit_bytes=56 * 1024 * 1024, collective_id=0, has_side_effects=True
        ),
    )(order, gate, seen, query, grad, key, value)


def shards(images_n, texts_n, queries, visual_keys, visual_values, out_grad, gate_value, image_order, image_seen):
    query_grad, key_share, value_share = attention(
        images_n, texts_n, image_order, gate_value, image_seen,
        queries[0], out_grad[0], visual_keys[0], visual_values[0]
    )
    return (query_grad[None], key_share[None], value_share[None])


def solution(mesh):
    placed = (
        P(None, "txt", "img"),
        P(None, "img", None),
        P(None, "img", None),
        P(None, "txt", "img"),
        P(None, "img"),
        P(),
        P("txt"),
    )
    return jax.shard_map(
        functools.partial(shards, mesh.shape["img"], mesh.shape["txt"]),
        mesh=mesh,
        in_specs=placed,
        out_specs=(P(None, "txt", "img"), P(None, "txt", "img"), P(None, "txt", "img")),
        check_vma=False,
    )
```

time: 84.9 us -> 75.3 us (0.89)
  Pallas kernels: 78.9 us -> 71.4 us
  local copies, waits for them, and re-layouts: 5.24 us -> 3.08 us
    pallas_call x1, Pallas kernels: 78.9 us -> 71.4 us  [attention(): pl.pallas_call(functools.partial(kernel, images_n, sides, relief), in_spe...]
    unnamed x7 -> x3, local copies, waits for them, and re-layouts: 5.24 us -> 3.08 us
where the time goes in v1:
time: 75.3 us; the launch traced here: 75.1 us
  Pallas kernels  71.4 us (95%)
  local copies, waits for them, and re-layouts  3.08 us (4%)
    pallas_call x1, Pallas kernels, attention(): pl.pallas_call(functools.partial(kernel, images_n, sides, relief), in_spe...  71.4 us
    unnamed x3, local copies, waits for them, and re-layouts  3.08 us

profile of v1, /device:TPU:0, one launch (start us, length us, event | category | flops | bytes accessed | tf_op | source)
XLA Modules:
  0.0 75.1 jit_solution(14048648305725160070)
XLA Ops:
  0.6 71.4 %shard_map.94 = (bf16[640,2048]{1,0:T(8,128)(2,1)S(1)}, f32[64,2048]{1,0:T(8,128)S(1)}, f32[64,2048]{1,0:T(8,128)S(1)}) custom-call(s32[1,8]{1,0:T(1,128)} %order_ref.1, f32[1,16]{1,0:T(1,128)} %gate_ref.1, s32[640]{0:T(1024)} %seen_ref.1, bf16[640,2048]{1,0:T(8,128)(2,1)} %bitcast.10, bf16[640,2048]{1,0:T(8,128)(2,1)} %bitcast.11, ...), custom_call_target="tpu_custom_call" | custom-call | tf_op jit(solution)/shard_map/pallas_call | solution.py:334
  72.0 1.5 %copy.13 = bf16[1,640,2048]{2,1,0:T(8,128)(2,1)} copy(bf16[1,640,2048]{2,1,0:T(8,128)(2,1)S(1)} %bitcast.7) | data formatting | bytes 5242880
  73.5 0.8 %copy.14 = f32[1,64,2048]{2,1,0:T(8,128)} copy(f32[1,64,2048]{2,1,0:T(8,128)S(1)} %bitcast.9) | data formatting | bytes 1048576
  74.3 0.8 %copy.15 = f32[1,64,2048]{2,1,0:T(8,128)} copy(f32[1,64,2048]{2,1,0:T(8,128)S(1)} %bitcast.8) | data formatting | bytes 1048576

commit v2 on v1

v2 whole, which is shorter than its diff:
```python
import functools
import math

import jax
import jax.numpy as jnp
from jax import lax
from jax.experimental import pallas as pl
from jax.experimental.pallas import tpu as pltpu
from jax.sharding import PartitionSpec as P

NT = (((1,), (1,)), ((), ()))
TN = (((0,), (0,)), ((), ()))
NN = (((1,), (0,)), ((), ()))
MESH = pl.DeviceIdType.MESH
LAGS = (2, 4, 6, 9)
RELIEF = 8
DEEP = (7, 11)


def matmul(left, right, dims):
    return lax.dot_general(left, right, dims, preferred_element_type=jnp.float32)


def head_grads(query, gated, key, value, bias):
    rows, tokens = key.shape[0], query.shape[0]
    images = bias.shape[0]
    scale = 1.0 / math.sqrt(query.shape[1])
    scores = matmul(key, query, NT) * (scale * math.log2(math.e))
    masked = (scores.reshape(images, rows // images, tokens) + bias[:, None, :]).reshape(rows, tokens)
    exponent = jnp.exp2(masked - jnp.max(masked, axis=0, keepdims=True))
    weights = exponent * (1.0 / jnp.sum(exponent, axis=0, keepdims=True))
    weight_half = weights.astype(jnp.bfloat16)
    weight_grad = matmul(value, gated, NT)
    delta = jnp.sum(weight_half.astype(jnp.float32) * weight_grad, axis=0, keepdims=True)
    score_half = (weights * (weight_grad - delta)).astype(jnp.bfloat16)
    query_grad = (matmul(key, score_half, TN) * scale).T
    key_grad = matmul(score_half, query, NN) * scale
    value_grad = matmul(weight_half, gated, NN)
    return query_grad, key_grad, value_grad


def kernel(images_n, sides, relief, deep, order_hbm, gate_hbm, seen_hbm, query_ref, grad_ref, key_ref, value_ref,
           out_ref, key_out, value_out,
           order_ref, gate_ref, seen_ref, bias, queries, grads, latents, full, pair_out, pair_in, edge_out, edge_in, near_out, near_in,
           far_out, far_in, deep_edge_out, deep_edge_in, deep_near_out, deep_near_in, deep_far_out, deep_far_in,
           load_sem, near_sem, far_sem, latent_send, pair_send, pair_recv, line_send, edge_recv, near_recv,
           far_recv, own_sem, ready):
    heads = gate_ref.shape[1]
    width = queries.shape[2]
    owned = key_ref.shape[0]
    half = jnp.bfloat16
    wide = jnp.float32
    pairs = sides // 2
    chips = images_n // 2
    me = lax.axis_index("img")
    place = lax.axis_index("txt")
    mine = place // 2
    side = place % 2
    other = 1 - side
    group = mine // 2
    parity = group % 2

    def hub_of(g):
        return g * 2 + (jnp.where(g < pairs // 2, 1, 0) if pairs > 1 else 1)

    hub = hub_of(group)
    rim = group * 4 + 1 - hub
    inner = mine == hub
    outer = mine == rim
    chip = me // 2
    sibling = chip * 2 + 1 - me % 2
    across = {"txt": mine * 2 + other}

    def at(z):
        return {"txt": z * 2 + side}

    def columns(index):
        return pl.ds(pl.multiple_of(index * width, width), width)

    def remote(src, dst, send, recv, device):
        return pltpu.make_async_remote_copy(src_ref=src, dst_ref=dst, send_sem=send, recv_sem=recv,
                                            device_id=device, device_id_type=MESH)

    def drain(ref, sem):
        pltpu.make_async_copy(ref, ref, sem).wait()

    def rows_of(owner, count):
        return pl.ds(pl.multiple_of(owner * owned, owned), count * owned)

    takes = jnp.where(inner, parity, 1 - parity)

    def relieved(index):
        return jnp.logical_and(index >= 1, index <= 2 * relief)

    def fetched(index):
        return jnp.logical_or(jnp.logical_not(relieved(index)), (index + 1) % 2 == takes)

    def forwarder(index):
        return jnp.logical_and(inner, jnp.logical_and(relieved(index), fetched(index)))

    def head_at(i):
        first = 2 * i - 1 + takes
        second = 2 * (i - relief) - takes
        return jnp.where(relieved(i), jnp.where(i <= relief, first, second), i)

    def due(t):
        low = jnp.where(relieved(t), 2 * (t - relief) - 1, t)
        high = jnp.where(relieved(t), jnp.where(t > relief, low + 2, low), t + 1)
        return low, high

    def is_deep(index):
        flag = index < 0
        for b in deep:
            flag = jnp.logical_or(flag, index == b)
        return flag

    def forward_copies(index):
        copies = []
        for device in (at(hub_of(group ^ 1)), at(rim)):
            for off in range(1, chips):
                view = latents.at[index, :, rows_of(((chip + off) % chips) * 2, 2), :]
                copies.append(remote(view, view, latent_send, far_sem.at[index], device))
        return copies

    def pair_copy(index, kind, count=sides):
        view = pl.ds(0, count)
        return remote(pair_out.at[index, kind, view], pair_in.at[index, kind, view],
                      pair_send, pair_recv.at[index, kind], across)

    def edge_copy(index, kind):
        return remote(edge_out.at[index, kind], edge_in.at[index, kind],
                      line_send, edge_recv.at[index, kind], at(hub))

    def near_copy(index, kind):
        return remote(near_out.at[index, kind], near_in.at[index, kind],
                      line_send, near_recv.at[index, kind], at(rim))

    def far_copy(index, kind, off, member):
        return remote(far_out.at[index, kind, off - 1, member], far_in.at[index, kind, off - 1],
                      line_send, far_recv.at[index, kind], at(((group + off) % pairs) * 2 + member))

    def slot(index):
        place = 0
        for n, b in enumerate(deep):
            place = jnp.where(index == b, n, place)
        return place

    def deep_edge_copy(index, kind):
        return remote(deep_edge_out.at[slot(index), kind], deep_edge_in.at[slot(index), kind],
                      line_send, edge_recv.at[index, kind], at(hub))

    def deep_near_copy(index, kind):
        return remote(deep_near_out.at[slot(index), kind], deep_near_in.at[slot(index), kind],
                      line_send, near_recv.at[index, kind], at(rim))

    def deep_far_copy(index, kind, off, member):
        return remote(deep_far_out.at[slot(index), kind, off - 1, member], deep_far_in.at[slot(index), kind, off - 1],
                      line_send, far_recv.at[index, kind], at(((group + off) % pairs) * 2 + member))

    barrier = pltpu.get_barrier_semaphore()

    def greet(device, semaphore=barrier):
        pl.semaphore_signal(semaphore, inc=1, device_id=device, device_id_type=MESH)

    for off in range(1, images_n):
        greet({"img": (me + off) % images_n})
    greet(across)
    greet(at(mine ^ 1))

    @pl.when(inner)
    def _():
        for off in range(1, pairs):
            greet(at(hub_of((group + off) % pairs)))

    small = [pltpu.make_async_copy(ref, buf, own_sem.at[n]) for n, (ref, buf) in enumerate(
        ((order_hbm, order_ref), (gate_hbm, gate_ref), (seen_hbm, seen_ref)))]

    def load(index):
        return [pltpu.make_async_copy(ref.at[:, columns(index)], buf.at[index], load_sem.at[index])
                for ref, buf in ((query_ref, queries), (grad_ref, grads))]

    for copy in small + load(0):
        copy.start()
    pl.semaphore_wait(barrier, images_n + 1 + (pairs - 1) * jnp.where(inner, 1, 0))

    @pl.when(inner)
    def _():
        for off in range(1, pairs):
            greet(at(hub_of((group + off) % pairs)), ready)

    sources = (key_ref, value_ref)

    def latent_copy(index, owner, kind, sem):
        return remote(sources[kind].at[:, columns(owner * heads + index)],
                      latents.at[index, kind, rows_of(me, 1), :],
                      latent_send, sem.at[index], {"img": owner})

    def send(index, carry):
        @pl.when(fetched(index))
        def _():
            for off in range(1, chips):
                for core in range(2):
                    for kind in range(2):
                        latent_copy(index, ((chip + off) % chips) * 2 + core, kind, far_sem).start()

        for kind, ref in enumerate(sources):
            latent_copy(index, sibling, kind, near_sem).start()
            pltpu.make_async_copy(ref.at[:, columns(me * heads + index)],
                                  latents.at[index, kind, rows_of(me, 1), :], near_sem.at[index]).start()

        @pl.when(index > 0)
        def _():
            for copy in load(index):
                copy.start()

        return carry

    lax.fori_loop(0, heads, send, 0)
    for copy in small:
        copy.wait()
    seen = seen_ref[...].reshape(1, bias.shape[1])
    for i in range(order_ref.shape[1]):
        bias[pl.ds(i, 1), :] = jnp.where(seen > order_ref[0, i], 0.0, -1e30)

    outs = (key_out, value_out)
    far_rows = pl.ds(0, (images_n - 2) * owned)

    def compute(index):
        drain(latents.at[index, :, pl.ds(0, 2 * owned), :], near_sem.at[index])
        drain(latents.at[index, :, far_rows, :], far_sem.at[index])

        @pl.when(forwarder(index))
        def _():
            for copy in forward_copies(index):
                copy.start()

        for copy in load(index):
            copy.wait()
        lane = lax.broadcasted_iota(jnp.int32, gate_ref.shape, 1)
        gate = jnp.sum(jnp.where(lane == index, gate_ref[...], 0.0), axis=1, keepdims=True)
        gated = (grads[index].astype(wide) * jnp.tanh(gate)).astype(half)
        query_grad, key_grad, value_grad = head_grads(
            queries[index], gated, latents[index, 0], latents[index, 1], bias[...]
        )
        out_ref[:, columns(index)] = query_grad.astype(out_ref.dtype)
        shape = full.shape[2:]
        full[index, 0] = key_grad.reshape(shape)
        full[index, 1] = value_grad.reshape(shape)

        @pl.when(jnp.logical_not(is_deep(index)))
        def _():
            for kind in (1, 0):
                for z in range(sides):
                    pair_out[index, kind, z] = full[index, kind, z * 2 + other].astype(half)
                pair_copy(index, kind).start()

        @pl.when(is_deep(index))
        def _():
            for kind in (1, 0):
                @pl.when(outer)
                def _():
                    for j in range(sides - 1):
                        for x in range(2):
                            deep_edge_out[slot(index), kind, j, x] = (
                                full[index, kind, ((rim + 1 + j) % sides) * 2 + x].astype(half)
                            )
                    deep_edge_copy(index, kind).start()

                @pl.when(inner)
                def _():
                    for x in range(2):
                        deep_near_out[slot(index), kind, x] = full[index, kind, rim * 2 + x].astype(half)
                    deep_near_copy(index, kind).start()

    def line(index, kind, z):
        return full[index, kind, z * 2 + side] + pair_in[index, kind, z].astype(wide)

    def relay(index, kind):
        pair_copy(index, kind).wait_recv()

        @pl.when(outer)
        def _():
            for j in range(sides - 1):
                edge_out[index, kind, j] = line(index, kind, (rim + 1 + j) % sides).astype(half)
            edge_copy(index, kind).start()

        @pl.when(inner)
        def _():
            near_out[index, kind] = line(index, kind, rim).astype(half)
            near_copy(index, kind).start()

        outs[kind][:, columns(index)] = line(index, kind, mine)

    mid = (hub - rim - 1 + sides) % sides

    def merge(index, kind):
        @pl.when(inner)
        def _():
            edge_copy(index, kind).wait_recv()
            for off in range(1, pairs):
                for member in range(2):
                    z = ((group + off) % pairs) * 2 + member
                    far_out[index, kind, off - 1, member] = (
                        line(index, kind, z) + edge_in[index, kind, (z - rim - 1 + sides) % sides].astype(wide)
                    ).astype(half)
                    far_copy(index, kind, off, member).start()
            outs[kind][:, columns(index)] += edge_in[index, kind, mid].astype(wide)

        @pl.when(outer)
        def _():
            near_copy(index, kind).wait_recv()
            outs[kind][:, columns(index)] += near_in[index, kind].astype(wide)

    def finish(index, kind):
        drain(far_in.at[index, kind], far_recv.at[index, kind])
        total = outs[kind][:, columns(index)]
        for off in range(1, pairs):
            total = total + far_in[index, kind, off - 1].astype(wide)
        outs[kind][:, columns(index)] = total

    def deep_merge(index, kind):
        @pl.when(inner)
        def _():
            deep_edge_copy(index, kind).wait_recv()
            for off in range(1, pairs):
                for member in range(2):
                    z = ((group + off) % pairs) * 2 + member
                    for x in range(2):
                        deep_far_out[slot(index), kind, off - 1, member, x] = (
                            full[index, kind, z * 2 + x]
                            + deep_edge_in[slot(index), kind, (z - rim - 1 + sides) % sides, x].astype(wide)
                        ).astype(half)
                    deep_far_copy(index, kind, off, member).start()
            for x in range(2):
                full[index, kind, mine * 2 + x] += deep_edge_in[slot(index), kind, mid, x].astype(wide)

        @pl.when(outer)
        def _():
            deep_near_copy(index, kind).wait_recv()
            for x in range(2):
                full[index, kind, mine * 2 + x] += deep_near_in[slot(index), kind, x].astype(wide)

    def deep_cross(index, kind):
        drain(deep_far_in.at[slot(index), kind], far_recv.at[index, kind])

        def total(x):
            value = full[index, kind, mine * 2 + x]
            for off in range(1, pairs):
                value = value + deep_far_in[slot(index), kind, off - 1, x].astype(wide)
            return value

        pair_out[index, kind, 0] = total(other).astype(half)
        pair_copy(index, kind, 1).start()
        outs[kind][:, columns(index)] = total(side)

    def deep_finish(index, kind):
        pair_copy(index, kind, 1).wait_recv()
        outs[kind][:, columns(index)] += pair_in[index, kind, 0].astype(wide)

    def both(index, plain, deeper):
        if plain is not None:
            @pl.when(jnp.logical_not(is_deep(index)))
            def _():
                for kind in (1, 0):
                    plain(index, kind)

        if deep and deeper is not None:
            @pl.when(is_deep(index))
            def _():
                for kind in (1, 0):
                    deeper(index, kind)

    def natural(t, plain, deeper):
        low, high = due(t)

        def one(index, carry):
            both(index, plain, deeper)
            return carry

        lax.fori_loop(low, high, one, 0)

    def step(i, carry):
        @pl.when(i < heads)
        def _():
            compute(head_at(i))

        @pl.when(i == LAGS[1])
        def _():
            @pl.when(inner)
            def _():
                pl.semaphore_wait(ready, pairs - 1)

        def after(lag, run):
            @pl.when(jnp.logical_and(i >= lag, i < heads + lag))
            def _():
                run(i - lag)

        after(LAGS[0], lambda t: both(head_at(t), relay, None))
        after(LAGS[1], lambda t: natural(t, merge, deep_merge))
        after(LAGS[2], lambda t: natural(t, finish, deep_cross))
        if deep:
            after(LAGS[3], lambda t: natural(t, None, deep_finish))
        return carry

    last = heads + LAGS[2]
    if deep:
        last = max(last, max(deep) + LAGS[3] + 1)
    lax.fori_loop(0, last, step, 0)

    plain = heads - len(deep)
    drain(latents.at[:, :, pl.ds(0, owned), :], latent_send)
    drain(latents.at[pl.ds(0, heads - relief), :, far_rows, :], latent_send)
    drain(pair_out.at[pl.ds(0, plain)], pair_send)
    if deep:
        drain(pair_out.at[pl.ds(0, len(deep)), :, pl.ds(0, 1)], pair_send)

    @pl.when(outer)
    def _():
        drain(edge_out.at[pl.ds(0, plain)], line_send)
        if deep:
            drain(deep_edge_out, line_send)

    @pl.when(inner)
    def _():
        if relief:
            drain(latents.at[pl.ds(0, 2 * relief), :, far_rows, :], latent_send)
        for ref in (near_out, far_out):
            drain(ref.at[pl.ds(0, plain)], line_send)
        if deep:
            for ref in (deep_near_out, deep_far_out):
                drain(ref, line_send)


def attention(images_n, texts_n, order, gate, seen, query, grad, key, value):
    tokens, width = query.shape
    heads = gate.shape[1]
    head_width = width // heads
    rows = key.shape[0] * images_n
    sides = texts_n // 2
    pairs = sides // 2
    share = rows // texts_n
    relief = heads // RELIEF if pairs % 2 == 0 and images_n > 2 else 0
    deep = tuple(heads * b // 16 for b in DEEP)
    vmem = pl.BlockSpec(memory_space=pltpu.VMEM)
    hbm = pl.BlockSpec(memory_space=pl.ANY)
    half = jnp.bfloat16
    dma = pltpu.SemaphoreType.DMA((heads,))
    kinds = pltpu.SemaphoreType.DMA((heads, 2))
    single = pltpu.SemaphoreType.DMA(())
    block = (share, head_width)
    units = (heads, 2)
    deeps = (max(len(deep), 1), 2)
    return pl.pallas_call(
        functools.partial(kernel, images_n, sides, relief, deep),
        in_specs=[hbm] * 7,
        out_specs=[vmem, vmem, vmem],
        out_shape=[pltpu.VMEM((tokens, width), half)] + [pltpu.VMEM((share, width), jnp.float32)] * 2,
        scratch_shapes=[
            pltpu.SMEM(order.shape, order.dtype), pltpu.VMEM(gate.shape, gate.dtype), pltpu.VMEM(seen.shape, seen.dtype),
            pltpu.VMEM((order.shape[1], tokens), jnp.float32),
            pltpu.VMEM((heads, tokens, head_width), half),
            pltpu.VMEM((heads, tokens, head_width), half),
            pltpu.VMEM((heads, 2, rows, head_width), half),
            pltpu.VMEM((*units, texts_n, *block), jnp.float32),
            pltpu.VMEM((*units, sides, *block), half),
            pltpu.VMEM((*units, sides, *block), half),
            pltpu.VMEM((*units, sides - 1, *block), half),
            pltpu.VMEM((*units, sides - 1, *block), half),
            pltpu.VMEM((*units, *block), half),
            pltpu.VMEM((*units, *block), half),
            pltpu.VMEM((*units, pairs - 1, 2, *block), half),
            pltpu.VMEM((*units, pairs - 1, *block), half),
            pltpu.VMEM((*deeps, sides - 1, 2, *block), half),
            pltpu.VMEM((*deeps, sides - 1, 2, *block), half),
            pltpu.VMEM((*deeps, 2, *block), half),
            pltpu.VMEM((*deeps, 2, *block), half),
            pltpu.VMEM((*deeps, pairs - 1, 2, 2, *block), half),
            pltpu.VMEM((*deeps, pairs - 1, 2, *block), half),
            dma, dma, dma, single, single, kinds, single, kinds, kinds, kinds,
            pltpu.SemaphoreType.DMA((3,)), pltpu.SemaphoreType.REGULAR,
        ],
        compiler_params=pltpu.CompilerParams(
            vmem_limit_bytes=56 * 1024 * 1024, collective_id=0, has_side_effects=True
        ),
    )(order, gate, seen, query, grad, key, value)


def publish(*arrays):
    def body(*refs):
        count = len(arrays)
        sems = refs[-1]
        copies = [pltpu.make_async_copy(refs[n], refs[count + n], sems.at[n]) for n in range(count)]
        for copy in copies:
            copy.start()
        for copy in copies:
            copy.wait()

    return pl.pallas_call(
        body,
        in_specs=[pl.BlockSpec(memory_space=pltpu.VMEM)] * len(arrays),
        out_specs=[pl.BlockSpec(memory_space=pl.ANY)] * len(arrays),
        out_shape=[jax.ShapeDtypeStruct(array.shape, array.dtype) for array in arrays],
        scratch_shapes=[pltpu.SemaphoreType.DMA((len(arrays),))],
        compiler_params=pltpu.CompilerParams(vmem_limit_bytes=1024 * 1024),
    )(*[pltpu.with_memory_space_constraint(array, pltpu.VMEM) for array in arrays])


def shards(images_n, texts_n, queries, visual_keys, visual_values, out_grad, gate_value, image_order, image_seen):
    query_grad, key_share, value_share = publish(*attention(
        images_n, texts_n, image_order, gate_value, image_seen,
        queries[0], out_grad[0], visual_keys[0], visual_values[0]
    ))
    return (query_grad[None], key_share[None], value_share[None])


def solution(mesh):
    placed = (
        P(None, "txt", "img"),
        P(None, "img", None),
        P(None, "img", None),
        P(None, "txt", "img"),
        P(None, "img"),
        P(),
        P("txt"),
    )
    return jax.shard_map(
        functools.partial(shards, mesh.shape["img"], mesh.shape["txt"]),
        mesh=mesh,
        in_specs=placed,
        out_specs=(P(None, "txt", "img"), P(None, "txt", "img"), P(None, "txt", "img")),
        check_vma=False,
    )
```

time: 75.3 us -> 66.7 us (0.89)
  Pallas kernels: 71.4 us -> 65.9 us
  local copies, waits for them, and re-layouts: 3.08 us -> 0 us
    pallas_call x1 -> x2, Pallas kernels: 71.4 us -> 65.9 us  [the longest x1 64.1 us: attention(): pl.pallas_call(functools.partial(kernel, images_n, sides, relief, deep),...]
    unnamed x3 -> x0, local copies, waits for them, and re-layouts: 3.08 us -> none
where the time goes in v2:
time: 66.7 us; the launch traced here: 66.6 us
  Pallas kernels  65.9 us (99%)
    pallas_call x1, Pallas kernels, attention(): pl.pallas_call(functools.partial(kernel, images_n, sides, relief, deep),...  64.1 us
    pallas_call x1, Pallas kernels, publish(): pl.pallas_call(body, in_specs=[pl.BlockSpec(memory_space=pltpu.VMEM)] * l...  1.86 us

profile of v2, /device:TPU:0, one launch (start us, length us, event | category | flops | bytes accessed | tf_op | source)
XLA Modules:
  0.0 66.6 jit_solution(2171011618525976206)
XLA Ops:
  0.6 64.1 %shard_map.94 = (bf16[640,2048]{1,0:T(8,128)(2,1)S(1)}, f32[64,2048]{1,0:T(8,128)S(1)}, f32[64,2048]{1,0:T(8,128)S(1)}) custom-call(s32[1,8]{1,0:T(1,128)} %order_hbm.1, f32[1,16]{1,0:T(1,128)} %gate_hbm.1, s32[640]{0:T(1024)} %seen_hbm.1, bf16[640,2048]{1,0:T(8,128)(2,1)} %bitcast.7, bf16[640,2048]{1,0:T(8,128)(2,1)} %bitcast.8, bf16[128,8192]{1,0:T(8,128)(2,1)} %bitcast.9, ...), custom_call_target="tpu_custom_call" | custom-call | tf_op jit(solution)/shard_map/pallas_call | solution.py:453
  64.7 1.9 %shard_map.95 = (bf16[640,2048]{1,0:T(8,128)(2,1)}, f32[64,2048]{1,0:T(8,128)}, f32[64,2048]{1,0:T(8,128)}) custom-call(bf16[640,2048]{1,0:T(8,128)(2,1)S(1)} %get-tuple-element.9.refs_0_, f32[64,2048]{1,0:T(8,128)S(1)} %get-tuple-element.10.refs_1_, f32[64,2048]{1,0:T(8,128)S(1)} %get-tuple-element.11.refs_2_), custom_call_target="tpu_custom_call" | custom-call | tf_op jit(solution)/shard_map/pallas_call | solution.py:498

commit v3 on v2

--- a/solution.py
+++ b/solution.py
@@ -12,9 +12,11 @@
 TN = (((0,), (0,)), ((), ()))
 NN = (((1,), (0,)), ((), ()))
 MESH = pl.DeviceIdType.MESH
-LAGS = (2, 4, 6, 9)
-RELIEF = 8
-DEEP = (7, 11)
+LAGS = (2, 4, 6)
+DEEP_LAGS = (2, 4, 7)
+RELIEF = 5
+DEEP = 8
+DIRECT = 1
 
 
 def matmul(left, right, dims):
@@ -39,12 +41,13 @@
     return query_grad, key_grad, value_grad
 
 
-def kernel(images_n, sides, relief, deep, order_hbm, gate_hbm, seen_hbm, query_ref, grad_ref, key_ref, value_ref,
+def kernel(images_n, sides, relief, direct, order_hbm, gate_hbm, seen_hbm, query_ref, grad_ref, key_ref, value_ref,
            out_ref, key_out, value_out,
            order_ref, gate_ref, seen_ref, bias, queries, grads, latents, full, pair_out, pair_in, edge_out, edge_in, near_out, near_in,
            far_out, far_in, deep_edge_out, deep_edge_in, deep_near_out, deep_near_in, deep_far_out, deep_far_in,
+           cross_out, cross_in, direct_out, direct_in, first,
            load_sem, near_sem, far_sem, latent_send, pair_send, pair_recv, line_send, edge_recv, near_recv,
-           far_recv, own_sem, ready):
+           far_recv, deep_line, deep_far, deep_cross_recv, direct_recv, own_sem, ready, open_line):
     heads = gate_ref.shape[1]
     width = queries.shape[2]
     owned = key_ref.shape[0]
@@ -108,11 +111,10 @@
         high = jnp.where(relieved(t), jnp.where(t > relief, low + 2, low), t + 1)
         return low, high
 
-    def is_deep(index):
-        flag = index < 0
-        for b in deep:
-            flag = jnp.logical_or(flag, index == b)
-        return flag
+    share = full.shape[3]
+    deep = cross_out.shape[2] if DEEP <= share // 8 else 0
+    top = pl.ds(0, share - deep)
+    bottom = pl.ds(share - deep, deep)
 
     def forward_copies(index):
         copies = []
@@ -122,10 +124,12 @@
                 copies.append(remote(view, view, latent_send, far_sem.at[index], device))
         return copies
 
-    def pair_copy(index, kind, count=sides):
-        view = pl.ds(0, count)
-        return remote(pair_out.at[index, kind, view], pair_in.at[index, kind, view],
+    def pair_copy(index, kind):
+        return remote(pair_out.at[index, kind], pair_in.at[index, kind],
                       pair_send, pair_recv.at[index, kind], across)
+
+    def cross_copy(index):
+        return remote(cross_out.at[index], cross_in.at[index], pair_send, deep_cross_recv.at[index], across)
 
     def edge_copy(index, kind):
         return remote(edge_out.at[index, kind], edge_in.at[index, kind],
@@ -139,23 +143,15 @@
         return remote(far_out.at[index, kind, off - 1, member], far_in.at[index, kind, off - 1],
                       line_send, far_recv.at[index, kind], at(((group + off) % pairs) * 2 + member))
 
-    def slot(index):
-        place = 0
-        for n, b in enumerate(deep):
-            place = jnp.where(index == b, n, place)
-        return place
-
-    def deep_edge_copy(index, kind):
-        return remote(deep_edge_out.at[slot(index), kind], deep_edge_in.at[slot(index), kind],
-                      line_send, edge_recv.at[index, kind], at(hub))
-
-    def deep_near_copy(index, kind):
-        return remote(deep_near_out.at[slot(index), kind], deep_near_in.at[slot(index), kind],
-                      line_send, near_recv.at[index, kind], at(rim))
-
-    def deep_far_copy(index, kind, off, member):
-        return remote(deep_far_out.at[slot(index), kind, off - 1, member], deep_far_in.at[slot(index), kind, off - 1],
-                      line_send, far_recv.at[index, kind], at(((group + off) % pairs) * 2 + member))
+    def deep_edge_copy(index):
+        return remote(deep_edge_out.at[index], deep_edge_in.at[index], line_send, deep_line.at[index], at(hub))
+
+    def deep_near_copy(index):
+        return remote(deep_near_out.at[index], deep_near_in.at[index], line_send, deep_line.at[index], at(rim))
+
+    def deep_far_copy(index, off, member):
+        return remote(deep_far_out.at[index, off - 1, member], deep_far_in.at[index, off - 1],
+                      line_send, deep_far.at[index], at(((group + off) % pairs) * 2 + member))
 
     barrier = pltpu.get_barrier_semaphore()
 
@@ -179,8 +175,13 @@
         return [pltpu.make_async_copy(ref.at[:, columns(index)], buf.at[index], load_sem.at[index])
                 for ref, buf in ((query_ref, queries), (grad_ref, grads))]
 
-    for copy in small + load(0):
+    sources = (key_ref, value_ref)
+    strangers = [((chip + off) % chips) * 2 + core for off in range(1, chips) for core in range(2)]
+    staged = [pltpu.make_async_copy(ref.at[:, columns(owner * heads)], first.at[n, kind], own_sem.at[3])
+              for n, owner in enumerate(strangers) for kind, ref in enumerate(sources)]
+    for copy in staged + small + load(0):
         copy.start()
+    drain(first, own_sem.at[3])
     pl.semaphore_wait(barrier, images_n + 1 + (pairs - 1) * jnp.where(inner, 1, 0))
 
     @pl.when(inner)
@@ -188,20 +189,18 @@
         for off in range(1, pairs):
             greet(at(hub_of((group + off) % pairs)), ready)
 
-    sources = (key_ref, value_ref)
-
-    def latent_copy(index, owner, kind, sem):
-        return remote(sources[kind].at[:, columns(owner * heads + index)],
+    def latent_copy(index, owner, kind, sem, source=None):
+        source = sources[kind].at[:, columns(owner * heads + index)] if source is None else source
+        return remote(source,
                       latents.at[index, kind, rows_of(me, 1), :],
                       latent_send, sem.at[index], {"img": owner})
 
     def send(index, carry):
-        @pl.when(fetched(index))
-        def _():
-            for off in range(1, chips):
-                for core in range(2):
-                    for kind in range(2):
-                        latent_copy(index, ((chip + off) % chips) * 2 + core, kind, far_sem).start()
+        @pl.when(jnp.logical_and(index > 0, fetched(index)))
+        def _():
+            for owner in strangers:
+                for kind in range(2):
+                    latent_copy(index, owner, kind, far_sem).start()
 
         for kind, ref in enumerate(sources):
             latent_copy(index, sibling, kind, near_sem).start()
@@ -215,6 +214,9 @@
 
         return carry
 
+    for n, owner in enumerate(strangers):
+        for kind in range(2):
+            latent_copy(0, owner, kind, far_sem, first.at[n, kind]).start()
     lax.fori_loop(0, heads, send, 0)
     for copy in small:
         copy.wait()
@@ -247,37 +249,57 @@
         full[index, 0] = key_grad.reshape(shape)
         full[index, 1] = value_grad.reshape(shape)
 
-        @pl.when(jnp.logical_not(is_deep(index)))
-        def _():
-            for kind in (1, 0):
-                for z in range(sides):
-                    pair_out[index, kind, z] = full[index, kind, z * 2 + other].astype(half)
-                pair_copy(index, kind).start()
-
-        @pl.when(is_deep(index))
-        def _():
-            for kind in (1, 0):
-                @pl.when(outer)
-                def _():
+        for kind in (1, 0):
+            for z in range(sides):
+                pair_out[index, kind, z] = full[index, kind, z * 2 + other, top].astype(half)
+            pair_copy(index, kind).start()
+        if deep:
+            @pl.when(outer)
+            def _():
+                for kind in range(2):
                     for j in range(sides - 1):
                         for x in range(2):
-                            deep_edge_out[slot(index), kind, j, x] = (
-                                full[index, kind, ((rim + 1 + j) % sides) * 2 + x].astype(half)
+                            deep_edge_out[index, j, x, kind] = (
+                                full[index, kind, ((rim + 1 + j) % sides) * 2 + x, bottom].astype(half)
                             )
-                    deep_edge_copy(index, kind).start()
-
-                @pl.when(inner)
-                def _():
+                deep_edge_copy(index).start()
+
+            @pl.when(inner)
+            def _():
+                for kind in range(2):
                     for x in range(2):
-                        deep_near_out[slot(index), kind, x] = full[index, kind, rim * 2 + x].astype(half)
-                    deep_near_copy(index, kind).start()
+                        deep_near_out[index, x, kind] = full[index, kind, rim * 2 + x, bottom].astype(half)
+                deep_near_copy(index).start()
 
     def line(index, kind, z):
-        return full[index, kind, z * 2 + side] + pair_in[index, kind, z].astype(wide)
+        return full[index, kind, z * 2 + side, top] + pair_in[index, kind, z].astype(wide)
+
+    def straight(index):
+        return index >= heads - direct
+
+    def direct_copy(index, kind, off):
+        n = index - (heads - direct)
+        return remote(direct_out.at[n, kind, off - 1], direct_in.at[n, kind, off - 1],
+                      line_send, direct_recv.at[n, kind], at((mine + off) % sides))
 
     def relay(index, kind):
         pair_copy(index, kind).wait_recv()
-
+        outs[kind][top, columns(index)] = line(index, kind, mine)
+
+        @pl.when(jnp.logical_not(straight(index)))
+        def _():
+            relay_plain(index, kind)
+
+        if direct:
+            @pl.when(straight(index))
+            def _():
+                for off in range(1, sides):
+                    direct_out[index - (heads - direct), kind, off - 1] = (
+                        line(index, kind, (mine + off) % sides).astype(half)
+                    )
+                    direct_copy(index, kind, off).start()
+
+    def relay_plain(index, kind):
         @pl.when(outer)
         def _():
             for j in range(sides - 1):
@@ -289,12 +311,10 @@
             near_out[index, kind] = line(index, kind, rim).astype(half)
             near_copy(index, kind).start()
 
-        outs[kind][:, columns(index)] = line(index, kind, mine)
-
     mid = (hub - rim - 1 + sides) % sides
 
     def merge(index, kind):
-        @pl.when(inner)
+        @pl.when(jnp.logical_and(inner, jnp.logical_not(straight(index))))
         def _():
             edge_copy(index, kind).wait_recv()
             for off in range(1, pairs):
@@ -304,77 +324,89 @@
                         line(index, kind, z) + edge_in[index, kind, (z - rim - 1 + sides) % sides].astype(wide)
                     ).astype(half)
                     far_copy(index, kind, off, member).start()
-            outs[kind][:, columns(index)] += edge_in[index, kind, mid].astype(wide)
-
-        @pl.when(outer)
+            outs[kind][top, columns(index)] += edge_in[index, kind, mid].astype(wide)
+
+        @pl.when(jnp.logical_and(outer, jnp.logical_not(straight(index))))
         def _():
             near_copy(index, kind).wait_recv()
-            outs[kind][:, columns(index)] += near_in[index, kind].astype(wide)
+            outs[kind][top, columns(index)] += near_in[index, kind].astype(wide)
+
+    def gather(index, kind, ref, count):
+        total = outs[kind][top, columns(index)]
+        for n in range(count):
+            total = total + ref[n].astype(wide)
+        outs[kind][top, columns(index)] = total
 
     def finish(index, kind):
-        drain(far_in.at[index, kind], far_recv.at[index, kind])
-        total = outs[kind][:, columns(index)]
-        for off in range(1, pairs):
-            total = total + far_in[index, kind, off - 1].astype(wide)
-        outs[kind][:, columns(index)] = total
-
-    def deep_merge(index, kind):
+        @pl.when(jnp.logical_not(straight(index)))
+        def _():
+            drain(far_in.at[index, kind], far_recv.at[index, kind])
+            gather(index, kind, far_in.at[index, kind], pairs - 1)
+
+        if direct:
+            @pl.when(straight(index))
+            def _():
+                n = index - (heads - direct)
+                drain(direct_in.at[n, kind], direct_recv.at[n, kind])
+                gather(index, kind, direct_in.at[n, kind], sides - 1)
+
+    def deep_merge(index):
         @pl.when(inner)
         def _():
-            deep_edge_copy(index, kind).wait_recv()
+            deep_edge_copy(index).wait_recv()
             for off in range(1, pairs):
                 for member in range(2):
                     z = ((group + off) % pairs) * 2 + member
-                    for x in range(2):
-                        deep_far_out[slot(index), kind, off - 1, member, x] = (
-                            full[index, kind, z * 2 + x]
-                            + deep_edge_in[slot(index), kind, (z - rim - 1 + sides) % sides, x].astype(wide)
-                        ).astype(half)
-                    deep_far_copy(index, kind, off, member).start()
-            for x in range(2):
-                full[index, kind, mine * 2 + x] += deep_edge_in[slot(index), kind, mid, x].astype(wide)
+                    for kind in range(2):
+                        for x in range(2):
+                            deep_far_out[index, off - 1, member, x, kind] = (
+                                full[index, kind, z * 2 + x, bottom]
+                                + deep_edge_in[index, (z - rim - 1 + sides) % sides, x, kind].astype(wide)
+                            ).astype(half)
+                    deep_far_copy(index, off, member).start()
+            for kind in range(2):
+                for x in range(2):
+                    full[index, kind, mine * 2 + x, bottom] += deep_edge_in[index, mid, x, kind].astype(wide)
 
         @pl.when(outer)
         def _():
-            deep_near_copy(index, kind).wait_recv()
-            for x in range(2):
-                full[index, kind, mine * 2 + x] += deep_near_in[slot(index), kind, x].astype(wide)
-
-    def deep_cross(index, kind):
-        drain(deep_far_in.at[slot(index), kind], far_recv.at[index, kind])
-
-        def total(x):
-            value = full[index, kind, mine * 2 + x]
+            deep_near_copy(index).wait_recv()
+            for kind in range(2):
+                for x in range(2):
+                    full[index, kind, mine * 2 + x, bottom] += deep_near_in[index, x, kind].astype(wide)
+
+    def deep_cross(index):
+        drain(deep_far_in.at[index], deep_far.at[index])
+
+        def total(kind, x):
+            value = full[index, kind, mine * 2 + x, bottom]
             for off in range(1, pairs):
-                value = value + deep_far_in[slot(index), kind, off - 1, x].astype(wide)
+                value = value + deep_far_in[index, off - 1, x, kind].astype(wide)
             return value
 
-        pair_out[index, kind, 0] = total(other).astype(half)
-        pair_copy(index, kind, 1).start()
-        outs[kind][:, columns(index)] = total(side)
-
-    def deep_finish(index, kind):
-        pair_copy(index, kind, 1).wait_recv()
-        outs[kind][:, columns(index)] += pair_in[index, kind, 0].astype(wide)
-
-    def both(index, plain, deeper):
-        if plain is not None:
-            @pl.when(jnp.logical_not(is_deep(index)))
-            def _():
-                for kind in (1, 0):
-                    plain(index, kind)
-
-        if deep and deeper is not None:
-            @pl.when(is_deep(index))
-            def _():
-                for kind in (1, 0):
-                    deeper(index, kind)
-
-    def natural(t, plain, deeper):
+        for kind in range(2):
+            cross_out[index, kind] = total(kind, other).astype(half)
+        cross_copy(index).start()
+        for kind in range(2):
+            outs[kind][bottom, columns(index)] = total(kind, side)
+
+    def deep_finish(index):
+        cross_copy(index).wait_recv()
+        for kind in range(2):
+            outs[kind][bottom, columns(index)] += cross_in[index, kind].astype(wide)
+
+    def kinds_of(run):
+        def each(index):
+            for kind in (1, 0):
+                run(index, kind)
+
+        return each
+
+    def natural(t, run):
         low, high = due(t)
 
         def one(index, carry):
-            both(index, plain, deeper)
+            run(index)
             return carry
 
         lax.fori_loop(low, high, one, 0)
@@ -384,39 +416,50 @@
         def _():
             compute(head_at(i))
 
-        @pl.when(i == LAGS[1])
+        @pl.when(i == min(LAGS[1], DEEP_LAGS[0]))
         def _():
             @pl.when(inner)
             def _():
                 pl.semaphore_wait(ready, pairs - 1)
+                if direct:
+                    greet(at(rim), open_line)
+
+            if direct:
+                @pl.when(outer)
+                def _():
+                    pl.semaphore_wait(open_line, 1)
 
         def after(lag, run):
+            if lag is None:
+                return
+
             @pl.when(jnp.logical_and(i >= lag, i < heads + lag))
             def _():
                 run(i - lag)
 
-        after(LAGS[0], lambda t: both(head_at(t), relay, None))
-        after(LAGS[1], lambda t: natural(t, merge, deep_merge))
-        after(LAGS[2], lambda t: natural(t, finish, deep_cross))
-        if deep:
-            after(LAGS[3], lambda t: natural(t, None, deep_finish))
+        after(DEEP_LAGS[0] if deep else None, lambda t: natural(t, deep_merge))
+        after(DEEP_LAGS[1] if deep else None, lambda t: natural(t, deep_cross))
+        after(LAGS[1], lambda t: natural(t, kinds_of(merge)))
+        after(LAGS[0], lambda t: kinds_of(relay)(head_at(t)))
+        after(LAGS[2], lambda t: natural(t, kinds_of(finish)))
+        after(DEEP_LAGS[2] if deep else None, lambda t: natural(t, deep_finish))
         return carry
 
-    last = heads + LAGS[2]
-    if deep:
-        last = max(last, max(deep) + LAGS[3] + 1)
+    last = heads + max(LAGS[2], DEEP_LAGS[2] if deep else 0)
     lax.fori_loop(0, last, step, 0)
 
-    plain = heads - len(deep)
     drain(latents.at[:, :, pl.ds(0, owned), :], latent_send)
     drain(latents.at[pl.ds(0, heads - relief), :, far_rows, :], latent_send)
-    drain(pair_out.at[pl.ds(0, plain)], pair_send)
-    if deep:
-        drain(pair_out.at[pl.ds(0, len(deep)), :, pl.ds(0, 1)], pair_send)
+    for ref in (pair_out, cross_out) if deep else (pair_out,):
+        drain(ref, pair_send)
+
+    plain = pl.ds(0, heads - direct)
+    if direct:
+        drain(direct_out, line_send)
 
     @pl.when(outer)
     def _():
-        drain(edge_out.at[pl.ds(0, plain)], line_send)
+        drain(edge_out.at[plain], line_send)
         if deep:
             drain(deep_edge_out, line_send)
 
@@ -424,11 +467,8 @@
     def _():
         if relief:
             drain(latents.at[pl.ds(0, 2 * relief), :, far_rows, :], latent_send)
-        for ref in (near_out, far_out):
-            drain(ref.at[pl.ds(0, plain)], line_send)
-        if deep:
-            for ref in (deep_near_out, deep_far_out):
-                drain(ref, line_send)
+        for ref in (near_out.at[plain], far_out.at[plain]) + ((deep_near_out, deep_far_out) if deep else ()):
+            drain(ref, line_send)
 
 
 def attention(images_n, texts_n, order, gate, seen, query, grad, key, value):
@@ -440,18 +480,19 @@
     pairs = sides // 2
     share = rows // texts_n
     relief = heads // RELIEF if pairs % 2 == 0 and images_n > 2 else 0
-    deep = tuple(heads * b // 16 for b in DEEP)
+    deep = DEEP if DEEP <= share // 8 else 0
     vmem = pl.BlockSpec(memory_space=pltpu.VMEM)
     hbm = pl.BlockSpec(memory_space=pl.ANY)
     half = jnp.bfloat16
     dma = pltpu.SemaphoreType.DMA((heads,))
     kinds = pltpu.SemaphoreType.DMA((heads, 2))
     single = pltpu.SemaphoreType.DMA(())
-    block = (share, head_width)
+    block = (share - deep, head_width)
+    direct = DIRECT if sides <= 4 else 0
+    small = (max(deep, 8), head_width)
     units = (heads, 2)
-    deeps = (max(len(deep), 1), 2)
     return pl.pallas_call(
-        functools.partial(kernel, images_n, sides, relief, deep),
+        functools.partial(kernel, images_n, sides, relief, direct),
         in_specs=[hbm] * 7,
         out_specs=[vmem, vmem, vmem],
         out_shape=[pltpu.VMEM((tokens, width), half)] + [pltpu.VMEM((share, width), jnp.float32)] * 2,
@@ -461,7 +502,7 @@
             pltpu.VMEM((heads, tokens, head_width), half),
             pltpu.VMEM((heads, tokens, head_width), half),
             pltpu.VMEM((heads, 2, rows, head_width), half),
-            pltpu.VMEM((*units, texts_n, *block), jnp.float32),
+            pltpu.VMEM((*units, texts_n, share, head_width), jnp.float32),
             pltpu.VMEM((*units, sides, *block), half),
             pltpu.VMEM((*units, sides, *block), half),
             pltpu.VMEM((*units, sides - 1, *block), half),
@@ -470,14 +511,20 @@
             pltpu.VMEM((*units, *block), half),
             pltpu.VMEM((*units, pairs - 1, 2, *block), half),
             pltpu.VMEM((*units, pairs - 1, *block), half),
-            pltpu.VMEM((*deeps, sides - 1, 2, *block), half),
-            pltpu.VMEM((*deeps, sides - 1, 2, *block), half),
-            pltpu.VMEM((*deeps, 2, *block), half),
-            pltpu.VMEM((*deeps, 2, *block), half),
-            pltpu.VMEM((*deeps, pairs - 1, 2, 2, *block), half),
-            pltpu.VMEM((*deeps, pairs - 1, 2, *block), half),
+            pltpu.VMEM((heads, sides - 1, 2, 2, *small), half),
+            pltpu.VMEM((heads, sides - 1, 2, 2, *small), half),
+            pltpu.VMEM((heads, 2, 2, *small), half),
+            pltpu.VMEM((heads, 2, 2, *small), half),
+            pltpu.VMEM((heads, pairs - 1, 2, 2, 2, *small), half),
+            pltpu.VMEM((heads, pairs - 1, 2, 2, *small), half),
+            pltpu.VMEM((*units, *small), half),
+            pltpu.VMEM((*units, *small), half),
+            pltpu.VMEM((max(direct, 1), 2, sides - 1, *block), half),
+            pltpu.VMEM((max(direct, 1), 2, sides - 1, *block), half),
+            pltpu.VMEM((images_n - 2, 2, rows // images_n, head_width), half),
             dma, dma, dma, single, single, kinds, single, kinds, kinds, kinds,
-            pltpu.SemaphoreType.DMA((3,)), pltpu.SemaphoreType.REGULAR,
+            dma, dma, dma, pltpu.SemaphoreType.DMA((max(direct, 1), 2)), pltpu.SemaphoreType.DMA((4,)),
+            pltpu.SemaphoreType.REGULAR, pltpu.SemaphoreType.REGULAR,
         ],
         compiler_params=pltpu.CompilerParams(
             vmem_limit_bytes=56 * 1024 * 1024, collective_id=0, has_side_effects=True

time: 66.7 us -> 64.2 us (0.963)
  Pallas kernels: 65.9 us -> 63.4 us
    pallas_call x1, Pallas kernels: 64.1 us -> 61.6 us  [attention(): pl.pallas_call(functools.partial(kernel, images_n, sides, relief, direct)...]
where the time goes in v3:
time: 64.2 us; the launch traced here: 64.1 us
  Pallas kernels  63.4 us (99%)
    pallas_call x1, Pallas kernels, attention(): pl.pallas_call(functools.partial(kernel, images_n, sides, relief, direct)...  61.6 us
    pallas_call x1, Pallas kernels, publish(): pl.pallas_call(body, in_specs=[pl.BlockSpec(memory_space=pltpu.VMEM)] * l...  1.86 us

profile of v3, /device:TPU:0, one launch (start us, length us, event | category | flops | bytes accessed | tf_op | source)
XLA Modules:
  0.0 64.1 jit_solution(7254305906531994535)
XLA Ops:
  0.6 61.6 %shard_map.94 = (bf16[640,2048]{1,0:T(8,128)(2,1)S(1)}, f32[64,2048]{1,0:T(8,128)S(1)}, f32[64,2048]{1,0:T(8,128)S(1)}) custom-call(s32[1,8]{1,0:T(1,128)} %order_hbm.1, f32[1,16]{1,0:T(1,128)} %gate_hbm.1, s32[640]{0:T(1024)} %seen_hbm.1, bf16[640,2048]{1,0:T(8,128)(2,1)} %bitcast.7, bf16[640,2048]{1,0:T(8,128)(2,1)} %bitcast.8, bf16[128,8192]{1,0:T(8,128)(2,1)} %bitcast.9, ...), custom_call_target="tpu_custom_call" | custom-call | tf_op jit(solution)/shard_map/pallas_call | solution.py:494
  62.2 1.9 %shard_map.95 = (bf16[640,2048]{1,0:T(8,128)(2,1)}, f32[64,2048]{1,0:T(8,128)}, f32[64,2048]{1,0:T(8,128)}) custom-call(bf16[640,2048]{1,0:T(8,128)(2,1)S(1)} %get-tuple-element.9.refs_0_, f32[64,2048]{1,0:T(8,128)S(1)} %get-tuple-element.10.refs_1_, f32[64,2048]{1,0:T(8,128)S(1)} %get-tuple-element.11.refs_2_), custom_call_target="tpu_custom_call" | custom-call | tf_op jit(solution)/shard_map/pallas_call | solution.py:545

commit v4 on v3

--- a/solution.py
+++ b/solution.py
@@ -46,7 +46,7 @@
            order_ref, gate_ref, seen_ref, bias, queries, grads, latents, full, pair_out, pair_in, edge_out, edge_in, near_out, near_in,
            far_out, far_in, deep_edge_out, deep_edge_in, deep_near_out, deep_near_in, deep_far_out, deep_far_in,
            cross_out, cross_in, direct_out, direct_in, first,
-           load_sem, near_sem, far_sem, latent_send, pair_send, pair_recv, line_send, edge_recv, near_recv,
+           load_sem, near_sem, far_sem, latent_send, pair_send, pair_recv, line_send, line_recv, last_recv,
            far_recv, deep_line, deep_far, deep_cross_recv, direct_recv, own_sem, ready, open_line):
     heads = gate_ref.shape[1]
     width = queries.shape[2]
@@ -124,24 +124,25 @@
                 copies.append(remote(view, view, latent_send, far_sem.at[index], device))
         return copies
 
-    def pair_copy(index, kind):
+    def pair_copy(index):
+        return remote(pair_out.at[index], pair_in.at[index], pair_send, pair_recv.at[index], across)
+
+    def last_copy(index, kind):
         return remote(pair_out.at[index, kind], pair_in.at[index, kind],
-                      pair_send, pair_recv.at[index, kind], across)
+                      pair_send, last_recv.at[index - (heads - direct), kind], across)
 
     def cross_copy(index):
         return remote(cross_out.at[index], cross_in.at[index], pair_send, deep_cross_recv.at[index], across)
 
-    def edge_copy(index, kind):
-        return remote(edge_out.at[index, kind], edge_in.at[index, kind],
-                      line_send, edge_recv.at[index, kind], at(hub))
-
-    def near_copy(index, kind):
-        return remote(near_out.at[index, kind], near_in.at[index, kind],
-                      line_send, near_recv.at[index, kind], at(rim))
-
-    def far_copy(index, kind, off, member):
-        return remote(far_out.at[index, kind, off - 1, member], far_in.at[index, kind, off - 1],
-                      line_send, far_recv.at[index, kind], at(((group + off) % pairs) * 2 + member))
+    def edge_copy(index):
+        return remote(edge_out.at[index], edge_in.at[index], line_send, line_recv.at[index], at(hub))
+
+    def near_copy(index):
+        return remote(near_out.at[index], near_in.at[index], line_send, line_recv.at[index], at(rim))
+
+    def far_copy(index, off, member):
+        return remote(far_out.at[index, off - 1, member], far_in.at[index, off - 1],
+                      line_send, far_recv.at[index], at(((group + off) % pairs) * 2 + member))
 
     def deep_edge_copy(index):
         return remote(deep_edge_out.at[index], deep_edge_in.at[index], line_send, deep_line.at[index], at(hub))
@@ -171,9 +172,12 @@
     small = [pltpu.make_async_copy(ref, buf, own_sem.at[n]) for n, (ref, buf) in enumerate(
         ((order_hbm, order_ref), (gate_hbm, gate_ref), (seen_hbm, seen_ref)))]
 
+    def rest(index):
+        return jnp.minimum(index, 1)
+
     def load(index):
-        return [pltpu.make_async_copy(ref.at[:, columns(index)], buf.at[index], load_sem.at[index])
-                for ref, buf in ((query_ref, queries), (grad_ref, grads))]
+        return [pltpu.make_async_copy(ref.at[:, columns(index)], buf.at[index], load_sem.at[n, rest(index)])
+                for n, (ref, buf) in enumerate(((query_ref, queries), (grad_ref, grads)))]
 
     sources = (key_ref, value_ref)
     strangers = [((chip + off) % chips) * 2 + core for off in range(1, chips) for core in range(2)]
@@ -193,19 +197,19 @@
         source = sources[kind].at[:, columns(owner * heads + index)] if source is None else source
         return remote(source,
                       latents.at[index, kind, rows_of(me, 1), :],
-                      latent_send, sem.at[index], {"img": owner})
+                      latent_send, sem, {"img": owner})
 
     def send(index, carry):
         @pl.when(jnp.logical_and(index > 0, fetched(index)))
         def _():
             for owner in strangers:
                 for kind in range(2):
-                    latent_copy(index, owner, kind, far_sem).start()
+                    latent_copy(index, owner, kind, far_sem.at[index]).start()
 
         for kind, ref in enumerate(sources):
-            latent_copy(index, sibling, kind, near_sem).start()
+            latent_copy(index, sibling, kind, near_sem.at[rest(index)]).start()
             pltpu.make_async_copy(ref.at[:, columns(me * heads + index)],
-                                  latents.at[index, kind, rows_of(me, 1), :], near_sem.at[index]).start()
+                                  latents.at[index, kind, rows_of(me, 1), :], near_sem.at[rest(index)]).start()
 
         @pl.when(index > 0)
         def _():
@@ -216,7 +220,7 @@
 
     for n, owner in enumerate(strangers):
         for kind in range(2):
-            latent_copy(0, owner, kind, far_sem, first.at[n, kind]).start()
+            latent_copy(0, owner, kind, far_sem.at[0], first.at[n, kind]).start()
     lax.fori_loop(0, heads, send, 0)
     for copy in small:
         copy.wait()
@@ -227,8 +231,22 @@
     outs = (key_out, value_out)
     far_rows = pl.ds(0, (images_n - 2) * owned)
 
-    def compute(index):
-        drain(latents.at[index, :, pl.ds(0, 2 * owned), :], near_sem.at[index])
+    def arrive(part, count):
+        drain(latents.at[pl.ds(0, count), :, pl.ds(0, 2 * owned), :], near_sem.at[part])
+        for n, buf in enumerate((queries, grads)):
+            drain(buf.at[pl.ds(0, count)], load_sem.at[n, part])
+
+    def compute(i):
+        index = head_at(i)
+
+        @pl.when(i == 0)
+        def _():
+            arrive(0, 1)
+
+        @pl.when(i == 1)
+        def _():
+            arrive(1, heads - 1)
+
         drain(latents.at[index, :, far_rows, :], far_sem.at[index])
 
         @pl.when(forwarder(index))
@@ -236,8 +254,6 @@
             for copy in forward_copies(index):
                 copy.start()
 
-        for copy in load(index):
-            copy.wait()
         lane = lax.broadcasted_iota(jnp.int32, gate_ref.shape, 1)
         gate = jnp.sum(jnp.where(lane == index, gate_ref[...], 0.0), axis=1, keepdims=True)
         gated = (grads[index].astype(wide) * jnp.tanh(gate)).astype(half)
@@ -252,7 +268,15 @@
         for kind in (1, 0):
             for z in range(sides):
                 pair_out[index, kind, z] = full[index, kind, z * 2 + other, top].astype(half)
-            pair_copy(index, kind).start()
+            if direct:
+                @pl.when(straight(index))
+                def _():
+                    last_copy(index, kind).start()
+
+        @pl.when(jnp.logical_not(straight(index)))
+        def _():
+            pair_copy(index).start()
+
         if deep:
             @pl.when(outer)
             def _():
@@ -282,73 +306,82 @@
         return remote(direct_out.at[n, kind, off - 1], direct_in.at[n, kind, off - 1],
                       line_send, direct_recv.at[n, kind], at((mine + off) % sides))
 
-    def relay(index, kind):
-        pair_copy(index, kind).wait_recv()
-        outs[kind][top, columns(index)] = line(index, kind, mine)
-
+    def relay(index):
         @pl.when(jnp.logical_not(straight(index)))
         def _():
-            relay_plain(index, kind)
+            pair_copy(index).wait_recv()
+
+            @pl.when(outer)
+            def _():
+                for kind in range(2):
+                    for j in range(sides - 1):
+                        edge_out[index, kind, j] = line(index, kind, (rim + 1 + j) % sides).astype(half)
+                edge_copy(index).start()
+
+            @pl.when(inner)
+            def _():
+                for kind in range(2):
+                    near_out[index, kind] = line(index, kind, rim).astype(half)
+                near_copy(index).start()
+
+            for kind in range(2):
+                outs[kind][top, columns(index)] = line(index, kind, mine)
 
         if direct:
             @pl.when(straight(index))
             def _():
-                for off in range(1, sides):
-                    direct_out[index - (heads - direct), kind, off - 1] = (
-                        line(index, kind, (mine + off) % sides).astype(half)
-                    )
-                    direct_copy(index, kind, off).start()
-
-    def relay_plain(index, kind):
-        @pl.when(outer)
-        def _():
-            for j in range(sides - 1):
-                edge_out[index, kind, j] = line(index, kind, (rim + 1 + j) % sides).astype(half)
-            edge_copy(index, kind).start()
-
-        @pl.when(inner)
-        def _():
-            near_out[index, kind] = line(index, kind, rim).astype(half)
-            near_copy(index, kind).start()
+                for kind in (1, 0):
+                    last_copy(index, kind).wait_recv()
+                    for off in range(1, sides):
+                        direct_out[index - (heads - direct), kind, off - 1] = (
+                            line(index, kind, (mine + off) % sides).astype(half)
+                        )
+                        direct_copy(index, kind, off).start()
+                    outs[kind][top, columns(index)] = line(index, kind, mine)
 
     mid = (hub - rim - 1 + sides) % sides
 
-    def merge(index, kind):
+    def merge(index):
         @pl.when(jnp.logical_and(inner, jnp.logical_not(straight(index))))
         def _():
-            edge_copy(index, kind).wait_recv()
+            edge_copy(index).wait_recv()
             for off in range(1, pairs):
                 for member in range(2):
                     z = ((group + off) % pairs) * 2 + member
-                    far_out[index, kind, off - 1, member] = (
-                        line(index, kind, z) + edge_in[index, kind, (z - rim - 1 + sides) % sides].astype(wide)
-                    ).astype(half)
-                    far_copy(index, kind, off, member).start()
-            outs[kind][top, columns(index)] += edge_in[index, kind, mid].astype(wide)
+                    for kind in range(2):
+                        far_out[index, off - 1, member, kind] = (
+                            line(index, kind, z) + edge_in[index, kind, (z - rim - 1 + sides) % sides].astype(wide)
+                        ).astype(half)
+                    far_copy(index, off, member).start()
+            for kind in range(2):
+                outs[kind][top, columns(index)] += edge_in[index, kind, mid].astype(wide)
 
         @pl.when(jnp.logical_and(outer, jnp.logical_not(straight(index))))
         def _():
-            near_copy(index, kind).wait_recv()
-            outs[kind][top, columns(index)] += near_in[index, kind].astype(wide)
-
-    def gather(index, kind, ref, count):
+            near_copy(index).wait_recv()
+            for kind in range(2):
+                outs[kind][top, columns(index)] += near_in[index, kind].astype(wide)
+
+    def gather(index, kind, terms):
         total = outs[kind][top, columns(index)]
-        for n in range(count):
-            total = total + ref[n].astype(wide)
+        for term in terms:
+            total = total + term.astype(wide)
         outs[kind][top, columns(index)] = total
 
-    def finish(index, kind):
+    def finish(index):
         @pl.when(jnp.logical_not(straight(index)))
         def _():
-            drain(far_in.at[index, kind], far_recv.at[index, kind])
-            gather(index, kind, far_in.at[index, kind], pairs - 1)
+            drain(far_in.at[index], far_recv.at[index])
+            for kind in range(2):
+                gather(index, kind, [far_in[index, n, kind] for n in range(pairs - 1)])
 
         if direct:
             @pl.when(straight(index))
             def _():
                 n = index - (heads - direct)
-                drain(direct_in.at[n, kind], direct_recv.at[n, kind])
-                gather(index, kind, direct_in.at[n, kind], sides - 1)
+                for kind in (1, 0):
+                    drain(direct_in.at[n, kind], direct_recv.at[n, kind])
+                    gather(index, kind, [direct_in[n, kind, off] for off in range(sides - 1)])
 
     def deep_merge(index):
         @pl.when(inner)
@@ -395,13 +428,6 @@
         for kind in range(2):
             outs[kind][bottom, columns(index)] += cross_in[index, kind].astype(wide)
 
-    def kinds_of(run):
-        def each(index):
-            for kind in (1, 0):
-                run(index, kind)
-
-        return each
-
     def natural(t, run):
         low, high = due(t)
 
@@ -414,7 +440,7 @@
     def step(i, carry):
         @pl.when(i < heads)
         def _():
-            compute(head_at(i))
+            compute(i)
 
         @pl.when(i == min(LAGS[1], DEEP_LAGS[0]))
         def _():
@@ -439,9 +465,9 @@
 
         after(DEEP_LAGS[0] if deep else None, lambda t: natural(t, deep_merge))
         after(DEEP_LAGS[1] if deep else None, lambda t: natural(t, deep_cross))
-        after(LAGS[1], lambda t: natural(t, kinds_of(merge)))
-        after(LAGS[0], lambda t: kinds_of(relay)(head_at(t)))
-        after(LAGS[2], lambda t: natural(t, kinds_of(finish)))
+        after(LAGS[1], lambda t: natural(t, merge))
+        after(LAGS[0], lambda t: relay(head_at(t)))
+        after(LAGS[2], lambda t: natural(t, finish))
         after(DEEP_LAGS[2] if deep else None, lambda t: natural(t, deep_finish))
         return carry
 
@@ -485,10 +511,12 @@
     hbm = pl.BlockSpec(memory_space=pl.ANY)
     half = jnp.bfloat16
     dma = pltpu.SemaphoreType.DMA((heads,))
-    kinds = pltpu.SemaphoreType.DMA((heads, 2))
+    two = pltpu.SemaphoreType.DMA((2, 2))
+    pair = pltpu.SemaphoreType.DMA((2,))
     single = pltpu.SemaphoreType.DMA(())
     block = (share - deep, head_width)
     direct = DIRECT if sides <= 4 else 0
+    last = pltpu.SemaphoreType.DMA((max(direct, 1), 2))
     small = (max(deep, 8), head_width)
     units = (heads, 2)
     return pl.pallas_call(
@@ -509,8 +537,8 @@
             pltpu.VMEM((*units, sides - 1, *block), half),
             pltpu.VMEM((*units, *block), half),
             pltpu.VMEM((*units, *block), half),
-            pltpu.VMEM((*units, pairs - 1, 2, *block), half),
-            pltpu.VMEM((*units, pairs - 1, *block), half),
+            pltpu.VMEM((heads, pairs - 1, 2, 2, *block), half),
+            pltpu.VMEM((heads, pairs - 1, 2, *block), half),
             pltpu.VMEM((heads, sides - 1, 2, 2, *small), half),
             pltpu.VMEM((heads, sides - 1, 2, 2, *small), half),
             pltpu.VMEM((heads, 2, 2, *small), half),
@@ -522,8 +550,8 @@
             pltpu.VMEM((max(direct, 1), 2, sides - 1, *block), half),
             pltpu.VMEM((max(direct, 1), 2, sides - 1, *block), half),
             pltpu.VMEM((images_n - 2, 2, rows // images_n, head_width), half),
-            dma, dma, dma, single, single, kinds, single, kinds, kinds, kinds,
-            dma, dma, dma, pltpu.SemaphoreType.DMA((max(direct, 1), 2)), pltpu.SemaphoreType.DMA((4,)),
+            two, pair, dma, single, single, dma, single, dma, last, dma,
+            dma, dma, dma, last, pltpu.SemaphoreType.DMA((4,)),
             pltpu.SemaphoreType.REGULAR, pltpu.SemaphoreType.REGULAR,
         ],
         compiler_params=pltpu.CompilerParams(

time: 64.2 us -> 63.8 us (level)
  no operation moved by 1% of the time
where the time goes in v4:
time: 63.8 us; the launch traced here: 63.7 us
  Pallas kernels  63 us (99%)
  between operations  0.64 us (1%)
    pallas_call x1, Pallas kernels, attention(): pl.pallas_call(functools.partial(kernel, images_n, sides, relief, direct)...  61.2 us
    pallas_call x1, Pallas kernels, publish(): pl.pallas_call(body, in_specs=[pl.BlockSpec(memory_space=pltpu.VMEM)] * l...  1.86 us

profile of v4, /device:TPU:0, one launch (start us, length us, event | category | flops | bytes accessed | tf_op | source)
XLA Modules:
  0.0 63.7 jit_solution(14527698573746744159)
XLA Ops:
  0.6 61.2 %shard_map.94 = (bf16[640,2048]{1,0:T(8,128)(2,1)S(1)}, f32[64,2048]{1,0:T(8,128)S(1)}, f32[64,2048]{1,0:T(8,128)S(1)}) custom-call(s32[1,8]{1,0:T(1,128)} %order_hbm.1, f32[1,16]{1,0:T(1,128)} %gate_hbm.1, s32[640]{0:T(1024)} %seen_hbm.1, bf16[640,2048]{1,0:T(8,128)(2,1)} %bitcast.7, bf16[640,2048]{1,0:T(8,128)(2,1)} %bitcast.8, bf16[128,8192]{1,0:T(8,128)(2,1)} %bitcast.9, ...), custom_call_target="tpu_custom_call" | custom-call | tf_op jit(solution)/shard_map/pallas_call | solution.py:522
  61.8 1.9 %shard_map.95 = (bf16[640,2048]{1,0:T(8,128)(2,1)}, f32[64,2048]{1,0:T(8,128)}, f32[64,2048]{1,0:T(8,128)}) custom-call(bf16[640,2048]{1,0:T(8,128)(2,1)S(1)} %get-tuple-element.9.refs_0_, f32[64,2048]{1,0:T(8,128)S(1)} %get-tuple-element.10.refs_1_, f32[64,2048]{1,0:T(8,128)S(1)} %get-tuple-element.11.refs_2_), custom_call_target="tpu_custom_call" | custom-call | tf_op jit(solution)/shard_map/pallas_call | solution.py:573

commit v5 on v4

--- a/solution.py
+++ b/solution.py
@@ -102,13 +102,17 @@
         return jnp.logical_and(inner, jnp.logical_and(relieved(index), fetched(index)))
 
     def head_at(i):
-        first = 2 * i - 1 + takes
-        second = 2 * (i - relief) - takes
-        return jnp.where(relieved(i), jnp.where(i <= relief, first, second), i)
+        k = i // 2
+        taken = jnp.where(i == 1, 1 + takes, 2 * k + 1 + takes)
+        handed = 2 * k - takes
+        late = jnp.logical_or(jnp.logical_and(i % 2 == 1, i > 1), i == 2 * relief)
+        return jnp.where(relieved(i), jnp.where(late, handed, taken), i)
 
     def due(t):
-        low = jnp.where(relieved(t), 2 * (t - relief) - 1, t)
-        high = jnp.where(relieved(t), jnp.where(t > relief, low + 2, low), t + 1)
+        k = t // 2
+        late = jnp.logical_or(jnp.logical_and(t % 2 == 1, t > 1), t == 2 * relief)
+        low = jnp.where(relieved(t), 2 * k - 1, t)
+        high = jnp.where(relieved(t), jnp.where(late, low + 2, low), t + 1)
         return low, high
 
     share = full.shape[3]

time: 63.8 us -> 63.2 us (level)
  Pallas kernels: 63 us -> 62.3 us
    pallas_call x1, Pallas kernels: 61.2 us -> 60.4 us  [attention(): pl.pallas_call(functools.partial(kernel, images_n, sides, relief, direct)...]
where the time goes in v5:
time: 63.2 us; the launch traced here: 62.9 us
  Pallas kernels  62.3 us (99%)
  between operations  0.64 us (1%)
    pallas_call x1, Pallas kernels, attention(): pl.pallas_call(functools.partial(kernel, images_n, sides, relief, direct)...  60.4 us
    pallas_call x1, Pallas kernels, publish(): pl.pallas_call(body, in_specs=[pl.BlockSpec(memory_space=pltpu.VMEM)] * l...  1.86 us

profile of v5, /device:TPU:0, one launch (start us, length us, event | category | flops | bytes accessed | tf_op | source)
XLA Modules:
  0.0 62.9 jit_solution(16682070461210708011)
XLA Ops:
  0.6 60.4 %shard_map.94 = (bf16[640,2048]{1,0:T(8,128)(2,1)S(1)}, f32[64,2048]{1,0:T(8,128)S(1)}, f32[64,2048]{1,0:T(8,128)S(1)}) custom-call(s32[1,8]{1,0:T(1,128)} %order_hbm.1, f32[1,16]{1,0:T(1,128)} %gate_hbm.1, s32[640]{0:T(1024)} %seen_hbm.1, bf16[640,2048]{1,0:T(8,128)(2,1)} %bitcast.7, bf16[640,2048]{1,0:T(8,128)(2,1)} %bitcast.8, bf16[128,8192]{1,0:T(8,128)(2,1)} %bitcast.9, ...), custom_call_target="tpu_custom_call" | custom-call | tf_op jit(solution)/shard_map/pallas_call | solution.py:526
  61.1 1.9 %shard_map.95 = (bf16[640,2048]{1,0:T(8,128)(2,1)}, f32[64,2048]{1,0:T(8,128)}, f32[64,2048]{1,0:T(8,128)}) custom-call(bf16[640,2048]{1,0:T(8,128)(2,1)S(1)} %get-tuple-element.9.refs_0_, f32[64,2048]{1,0:T(8,128)S(1)} %get-tuple-element.10.refs_1_, f32[64,2048]{1,0:T(8,128)S(1)} %get-tuple-element.11.refs_2_), custom_call_target="tpu_custom_call" | custom-call | tf_op jit(solution)/shard_map/pallas_call | solution.py:577

commit v6 on v5

--- a/solution.py
+++ b/solution.py
@@ -336,7 +336,7 @@
             def _():
                 for kind in (1, 0):
                     last_copy(index, kind).wait_recv()
-                    for off in range(1, sides):
+                    for off in sorted(range(1, sides), key=lambda o: abs(o - sides // 2)):
                         direct_out[index - (heads - direct), kind, off - 1] = (
                             line(index, kind, (mine + off) % sides).astype(half)
                         )

time: 63.2 us -> 63.2 us (level)
  no operation moved by 1% of the time
where the time goes in v6:
time: 63.2 us; the launch traced here: 62.9 us
  Pallas kernels  62.3 us (99%)
  between operations  0.64 us (1%)
    pallas_call x1, Pallas kernels, attention(): pl.pallas_call(functools.partial(kernel, images_n, sides, relief, direct)...  60.4 us
    pallas_call x1, Pallas kernels, publish(): pl.pallas_call(body, in_specs=[pl.BlockSpec(memory_space=pltpu.VMEM)] * l...  1.86 us

profile of v6, /device:TPU:0, one launch (start us, length us, event | category | flops | bytes accessed | tf_op | source)
XLA Modules:
  0.0 62.9 jit_solution(17336208731165964271)
XLA Ops:
  0.6 60.4 %shard_map.94 = (bf16[640,2048]{1,0:T(8,128)(2,1)S(1)}, f32[64,2048]{1,0:T(8,128)S(1)}, f32[64,2048]{1,0:T(8,128)S(1)}) custom-call(s32[1,8]{1,0:T(1,128)} %order_hbm.1, f32[1,16]{1,0:T(1,128)} %gate_hbm.1, s32[640]{0:T(1024)} %seen_hbm.1, bf16[640,2048]{1,0:T(8,128)(2,1)} %bitcast.7, bf16[640,2048]{1,0:T(8,128)(2,1)} %bitcast.8, bf16[128,8192]{1,0:T(8,128)(2,1)} %bitcast.9, ...), custom_call_target="tpu_custom_call" | custom-call | tf_op jit(solution)/shard_map/pallas_call | solution.py:526
  61.1 1.9 %shard_map.95 = (bf16[640,2048]{1,0:T(8,128)(2,1)}, f32[64,2048]{1,0:T(8,128)}, f32[64,2048]{1,0:T(8,128)}) custom-call(bf16[640,2048]{1,0:T(8,128)(2,1)S(1)} %get-tuple-element.9.refs_0_, f32[64,2048]{1,0:T(8,128)S(1)} %get-tuple-element.10.refs_1_, f32[64,2048]{1,0:T(8,128)S(1)} %get-tuple-element.11.refs_2_), custom_call_target="tpu_custom_call" | custom-call | tf_op jit(solution)/shard_map/pallas_call | solution.py:577
